TPU v7x, 32 devices: a whole 2x2x4 slice. The times are simulated.
32 devices in a mesh: row: 8 (over z, x), gz: 4 (over y, core).
Axes of the slice: x: 2, y: 2, z: 4, core: 2. Of those that a mesh axis runs over, the one named last changes fastest.
Arguments:
- state: float32 [4, 1024, 16, 2048], P(None, 'row', 'gz'), may hold values from -12 to 12, as said below
- green: bfloat16 [8, 1024, 1024], P('row'), may hold values from -1 to 5
- vertical: float32 [16, 16], replicated, may hold values from 0 to 1
Outputs:
- new_state: float32 [4, 1024, 16, 2048], P(None, 'row', 'gz')
- potential: float32 [1024, 16, 2048], P('row', 'gz')
Inputs may be any that keep to these rules, and one draw needn't show every extreme that they name: `state`: component 0 lies in 0.25 to 4; components 1 and 2 are at most 3 times component 0 in magnitude; component 3 lies between 0 and component 0.
All inputs are finite; a program needn't handle non-finite values.
Results may differ from a plain program's by a relative error of at most 0.0019.
Values may be sent and summed in bfloat16 or wider, within the bound.
No kernel may reach another device: no remote copies, remote signals or barrier semaphores. Data moves between devices by JAX's collectives and lax.ppermute only.
A program may use at most 192 MiB of HBM per device.

v0:
```python
import math

import jax
import jax.numpy as jnp
from jax import lax
from jax.sharding import PartitionSpec as P

sound_sq = 1.0
inner_radius = 1.0
radial_span = 4.0
courant = 0.2
precise = lax.Precision.HIGHEST


def padded_2(cells, sides, width):
    for axis, dim in sides:
        count = lax.axis_size(axis)
        ends = count - 1
        head = lax.slice_in_dim(cells, 0, width, axis=dim)
        tail = lax.slice_in_dim(cells, cells.shape[dim] - width, cells.shape[dim], axis=dim)
        cells = jnp.concatenate(
            [
                lax.ppermute(tail, axis, [(i, (i + 1) % count) for i in range(ends)]),
                cells,
                lax.ppermute(head, axis, [((i + 1) % count, i) for i in range(ends)]),
            ],
            axis=dim,
        )
    return cells


def mode_table(azimuth, modes):
    angle_index = (
        jnp.arange(azimuth, dtype=jnp.int32)[:, None]
        * jnp.arange(modes, dtype=jnp.int32)[None, :]
        % azimuth
    )
    angles = angle_index.astype(jnp.float32) * (2.0 * math.pi / azimuth)
    forward = jnp.concatenate([jnp.cos(angles), -jnp.sin(angles)], axis=1)
    weights = jnp.where(jnp.arange(modes) == 0, 1.0, 2.0) / azimuth
    weights = jnp.concatenate([weights, weights]).astype(jnp.float32)
    inverse = forward.T * weights[:, None]
    return (forward, inverse)


def minmod(former, latter):
    return jnp.where(
        former * latter > 0, jnp.where(jnp.abs(former) < jnp.abs(latter), former, latter), 0.0
    )


def rusanov(left_state, right_state, normal):
    onehot = (jnp.arange(4) == normal).astype(left_state.dtype).reshape(4, 1, 1, 1)

    def flux_of(values):
        velocity = values[normal] / values[0]
        return (values * velocity + sound_sq * values[0] * onehot, jnp.abs(velocity))

    flux_left, speed_left = flux_of(left_state)
    flux_right, speed_right = flux_of(right_state)
    reach = jnp.maximum(speed_left, speed_right) + math.sqrt(sound_sq)
    return 0.5 * (flux_left + flux_right) - 0.5 * reach * (right_state - left_state)


def advance(padded, potential, radial_slope, centres, radial_step):
    azimuth = padded.shape[-1]
    phi_step = 2.0 * math.pi / azimuth
    step_time = courant * min(radial_step, inner_radius * phi_step)
    slopes = minmod(padded[:, 1:-1] - padded[:, :-2], padded[:, 2:] - padded[:, 1:-1])
    centre_cells = padded[:, 1:-1]
    flux_radial = rusanov(
        centre_cells[:, :-1] + 0.5 * slopes[:, :-1], centre_cells[:, 1:] - 0.5 * slopes[:, 1:], 1
    )
    interior = padded[:, 2:-2]
    phi_slopes = minmod(
        interior - jnp.roll(interior, 1, axis=3), jnp.roll(interior, -1, axis=3) - interior
    )
    flux_phi = rusanov(
        interior + 0.5 * phi_slopes, jnp.roll(interior - 0.5 * phi_slopes, -1, axis=3), 2
    )
    face_radii = jnp.concatenate(
        [centres - 0.5 * radial_step, centres[-1:] + 0.5 * radial_step]
    ).reshape(1, -1, 1, 1)
    weighted = face_radii * flux_radial
    radius = centres.reshape(1, -1, 1, 1)
    tendency = (
        -(
            (weighted[:, 1:] - weighted[:, :-1]) / radial_step
            + (flux_phi - jnp.roll(flux_phi, 1, axis=3)) / phi_step
        )
        / radius
    )
    density = interior[0]
    spin = interior[2] / density
    radius_cells = centres.reshape(-1, 1, 1)
    azimuth_slope = (jnp.roll(potential, -1, axis=2) - jnp.roll(potential, 1, axis=2)) / (
        2.0 * phi_step
    )
    force_radial = (interior[2] * spin + sound_sq * density) / radius_cells - density * radial_slope
    force_phi = -(interior[1] * spin + density * azimuth_slope) / radius_cells
    zeros = jnp.zeros_like(density)
    sources = jnp.stack([zeros, force_radial, force_phi, zeros])
    return interior + step_time * (tendency + sources)


def mend_edges(padded, width, axis_dim):
    length = padded.shape[axis_dim]
    position = lax.axis_index("row")
    last_rank = lax.axis_size("row") - 1
    low_rim = lax.slice_in_dim(padded, 0, width, axis=axis_dim)
    middle = lax.slice_in_dim(padded, width, length - width, axis=axis_dim)
    high_rim = lax.slice_in_dim(padded, length - width, length, axis=axis_dim)
    first_cell = lax.slice_in_dim(middle, 0, 1, axis=axis_dim)
    last_cell = lax.slice_in_dim(
        middle, middle.shape[axis_dim] - 1, middle.shape[axis_dim], axis=axis_dim
    )
    low_rim = jnp.where(position == 0, jnp.broadcast_to(first_cell, low_rim.shape), low_rim)
    high_rim = jnp.where(
        position == last_rank, jnp.broadcast_to(last_cell, high_rim.shape), high_rim
    )
    return jnp.concatenate([low_rim, middle, high_rim], axis=axis_dim)


def body(state, green, vertical):
    radii, planes, azimuth = (state.shape[1], state.shape[2], state.shape[3])
    modes_dev, radial_all = (green.shape[0], green.shape[1])
    modes = modes_dev * lax.axis_size("row")
    radial_step = radial_span / radial_all
    forward, inverse = mode_table(azimuth, modes)
    padded_state = mend_edges(padded_2(state, (("row", 1),), 2), 2, 1)
    spectrum = jnp.dot(
        state[0].reshape(-1, azimuth),
        forward,
        precision=precise,
        preferred_element_type=jnp.float32,
    ).reshape(radii, planes, 2, modes)
    plane_start = lax.axis_index("gz") * planes
    column_all = lax.all_gather(spectrum, "gz", axis=1, tiled=True)
    own_rows = lax.dynamic_slice_in_dim(vertical, plane_start, planes, 0)
    mixed = jnp.einsum("zy,ryck->rzck", own_rows, column_all, precision=precise)
    mixed_b = mixed.astype(jnp.bfloat16)
    pot_modes = jnp.einsum(
        "mrs,skcm->rkcm",
        green,
        lax.all_to_all(mixed_b, "row", split_axis=3, concat_axis=0, tiled=True),
        preferred_element_type=jnp.float32,
    )
    pot_spec = lax.all_to_all(pot_modes, "row", split_axis=0, concat_axis=3, tiled=True)
    potential = jnp.dot(
        pot_spec.reshape(-1, 2 * modes),
        inverse,
        precision=precise,
        preferred_element_type=jnp.float32,
    ).reshape(radii, planes, azimuth)
    padded_pot = mend_edges(padded_2(potential, (("row", 0),), 1), 1, 0)
    radial_slope = (padded_pot[2:] - padded_pot[:-2]) / (2.0 * radial_step)
    offsets = (lax.axis_index("row") * radii + jnp.arange(radii, dtype=jnp.int32)).astype(
        jnp.float32
    )
    centres = inner_radius + (offsets + 0.5) * radial_step
    new_state = advance(padded_state, potential, radial_slope, centres, radial_step)
    return (new_state, potential)


def solution(mesh):
    placed = (P(None, "row", "gz", None), P("row", None, None), P())
    return jax.shard_map(
        body,
        mesh=mesh,
        in_specs=placed,
        out_specs=(P(None, "row", "gz", None), P("row", "gz", None)),
        check_vma=False,
    )
```

profile of v0, /device:TPU:0, one launch (start us, length us, event | category | flops | bytes accessed | tf_op | source)
XLA Modules:
  0.0 372.2 jit_solution(9035244303444112443)
XLA Ops:
  4.0 6.2 %collective-permute-start = (f32[4,2,4,2048]{3,2,1,0:T(4,128)}, f32[4,2,4,2048]{3,2,1,0:T(4,128)}, u32[]{:S(2)}, u32[]{:S(2)}) collective-permute-start(f32[4,2,4,2048]{3,2,1,0:T(4,128)} %get-tuple-element.18), channel_id=1, source_target_pairs={{0,4},{4,8},{8,12},{12,16},{16,20},{20,24},{24,28},{1,5},{5,9},{9,... | collective-permute-start | bytes 786440 | tf_op jit(solution)/shard_map/ppermute | solution.py:23
  10.5 4.8 %slice.180 = f32[1,128,4,2048]{3,2,1,0:T(4,128)} slice(f32[4,128,4,2048]{3,2,1,0:T(4,128)} %param.3), slice={[0:1], [0:128], [0:4], [0:2048]} | slice | bytes 8388608 | tf_op jit(solution)/shard_map/slice | solution.py:93
  15.2 5.3 %reshape_squeeze.3 = f32[512,2048]{1,0:T(8,128)} reshape(f32[1,128,4,2048]{3,2,1,0:T(4,128)} %slice.180) | data formatting | bytes 8388608 | tf_op jit(solution)/shard_map/reshape;squeeze | solution.py:132
  20.5 5.7 %convolution_bitcast_fusion = f32[512,16]{0,1:T(8,128)S(1)} fusion(f32[512,2048]{1,0:T(8,128)} %reshape_squeeze.3, f32[2048,8]{0,1:T(8,128)S(1)} %get-tuple-element.32, f32[2048,8]{0,1:T(8,128)S(1)} %get-tuple-element.33), kind=kOutput, calls=%fused_computation.68 | convolution fusion | flops 201359360 | bytes 4358144 | tf_op jit(solution)/shard_map/dot_general | solution.py:131
  27.0 5.6 %all_gather.3 = f32[128,16,2,8]{0,3,2,1:T(8,128)S(1)} all-gather(f32[128,4,2,8]{0,3,2,1:T(8,128)S(1)} %copy.16), channel_id=1, replica_groups=mesh['row'=8,'gz'=4] {'gz'}, dimensions={1}, use_global_device_ids=true | all-gather | bytes 163840 | tf_op jit(solution)/shard_map/all_gather | solution.py:138
  34.1 5.6 %all-to-all-start = ((bf16[128,4,2,8]{0,1,2,3:T(4,128)(2,1)}), bf16[128,4,2,8]{0,1,2,3:T(4,128)(2,1)S(1)}, u32[]{:S(2)}, u32[]{:S(2)}) async-start(bf16[128,4,2,8]{0,1,2,3:T(4,128)(2,1)} %copy.18), calls=%async_computation | async-start | bytes 32768 | tf_op jit(solution)/shard_map/all_to_all | solution.py:145
  42.3 27.3 %fusion.55 = (f32[4,128,4,2047]{3,2,1,0:T(4,128)}, f32[4,128,4,2047]{3,2,1,0:T(4,128)}) fusion(f32[4,128,4,2048]{3,2,1,0:T(4,128)} %param.3), kind=kLoop, calls=%fused_computation.117 | loop fusion | bytes 67076096 | tf_op jit(solution)/shard_map/jit(_roll_static)/slice | solution.py:76
  72.8 29.8 %fusion.50 = (f32[4,128,4,2048]{3,2,1,0:T(4,128)}, f32[4,128,4,2048]{3,2,1,0:T(4,128)}) fusion(f32[4,128,4,2048]{3,2,1,0:T(4,128)} %param.3, f32[4,128,4,1]{3,2,1,0:T(4,128)} %get-tuple-element.21, f32[4,128,4,2047]{3,2,1,0:T(4,128)} %get-tuple-element.23, f32[4,128,4,2047]{3,2,1,0:T(4,128)} %get-tuple-element.22, f32[4,128,4,1]{3,2,1,0:T(4,128)S(1)} %get-tuple-element.20), kind=kLoop, calls=%fused_computation.113 | loop fusion | flops 58720256 | bytes 83886080 | tf_op jit(solution)/shard_map/sub | solution.py:79
  102.6 12.4 %slice.206 = f32[4,128,4,2047]{3,2,1,0:T(4,128)S(1)} slice(f32[4,128,4,2048]{3,2,1,0:T(4,128)} %get-tuple-element.4), slice={[0:4], [0:128], [0:4], [1:2048]} | slice | bytes 33538048 | tf_op jit(solution)/shard_map/jit(_roll_static)/slice | solution.py:79
  121.1 12.8 %multiply_bitcast_fusion.1 = (f32[128,4,2048]{2,1,0:T(4,128)}, f32[1,128,4,2048]{3,2,1,0:T(4,128)}, f32[128,4,2048]{2,1,0:T(4,128)}, f32[128,4,2048]{2,1,0:T(4,128)}, f32[128,4,2048]{2,1,0:T(4,128)}) fusion(f32[4,128,4,2048]{3,2,1,0:T(4,128)} %get-tuple-element.5, f32[4,128,4,1]{3,2,1,0:T(4,128)S(1)} %slice.207, f32[4,128,4,2047]{3,2,1,0:T(4,128)S(1)} %slice.206), kind=kLoop, calls=%fused_computation.60 | loop fusion | flops 10485760 | bytes 46137344 | tf_op jit(solution)/shard_map/mul | solution.py:62
  133.9 25.8 %multiply_subtract_fusion = f32[4,128,4,2048]{3,2,1,0:T(4,128)} fusion(f32[4,128,4,2048]{3,2,1,0:T(4,128)} %get-tuple-element.5, f32[4,128,4,1]{3,2,1,0:T(4,128)S(1)} %slice.207, f32[4,128,4,2047]{3,2,1,0:T(4,128)} %copy-done.2, f32[128,4,2048]{2,1,0:T(4,128)} %get-tuple-element.2, f32[128,4,2048]{2,1,0:T(4,128)} %get-tuple-element.8, ...), kind=kLoop, calls=%fused_computation.31 | loop fusion | flops 50331648 | bytes 71303184 | tf_op jit(solution)/shard_map/sub | solution.py:62
  168.3 6.0 %all-to-all-start.1 = ((f32[8,1,1024]{2,1,0:T(1,128)}), f32[8,1,1024]{2,1,0:T(1,128)S(1)}, u32[]{:S(2)}, u32[]{:S(2)}) async-start(f32[8,1,1024]{2,1,0:T(1,128)} %reshape.122), calls=%async_computation.1 | async-start | bytes 65536 | tf_op jit(solution)/shard_map/all_to_all | solution.py:148
  175.1 5.9 %all-to-all-done.1 = f32[8,1,1024]{2,1,0:T(1,128)S(1)} async-done(((f32[8,1,1024]{2,1,0:T(1,128)}), f32[8,1,1024]{2,1,0:T(1,128)S(1)}, u32[]{:S(2)}, u32[]{:S(2)}) %all-to-all-start.1) | async-done | bytes 32800 | tf_op jit(solution)/shard_map/all_to_all | solution.py:148
  185.9 3.5 fusion.30
  191.4 5.2 %reshape.119 = f32[128,4,2048]{2,1,0:T(4,128)} reshape(f32[512,2048]{1,0:T(8,128)} %copy-done.5) | data formatting | bytes 8388608 | tf_op jit(solution)/shard_map/reshape | solution.py:154
  196.6 9.1 %slice_bitcast_fusion = (f32[1,128,4,2047]{3,2,1,0:T(4,128)}, f32[1,128,4,2047]{3,2,1,0:T(4,128)}) fusion(f32[128,4,2048]{2,1,0:T(4,128)} %reshape.119), kind=kLoop, calls=%fused_computation.46 | loop fusion | bytes 16769024 | tf_op jit(solution)/shard_map/jit(_roll_static)/concatenate | solution.py:96
  208.3 4.5 %collective-permute-start.3 = (f32[1,4,2048]{2,1,0:T(4,128)S(1)}, f32[1,4,2048]{2,1,0:T(4,128)S(1)}, u32[]{:S(2)}, u32[]{:S(2)}) collective-permute-start(f32[1,4,2048]{2,1,0:T(4,128)S(1)} %get-tuple-element.27), channel_id=1, source_target_pairs={{0,4},{4,8},{8,12},{12,16},{16,20},{20,24},{24,28},{1,5},{5,9},{9,... | collective-permute-start | bytes 98312 | tf_op jit(solution)/shard_map/ppermute | solution.py:23
  213.5 12.1 %fusion.21 = f32[1,128,4,2048]{3,2,1,0:T(4,128)} fusion(f32[1,128,4,1]{3,2,1,0:T(4,128)S(1)} %copy.23, f32[1,128,4,2047]{3,2,1,0:T(4,128)} %get-tuple-element.31, f32[1,128,4,2047]{3,2,1,0:T(4,128)} %get-tuple-element.30, f32[1,128,4,1]{3,2,1,0:T(4,128)S(1)} %copy.25, f32[4,128,4,2048]{3,2,1,0:T(4,128)} %param.3, f32[128]{0:T(128)S(1)} %copy-done.7), kind=kLoop, calls=%fused_computation.59 | loop fusion | flops 10485760 | bytes 25166336 | tf_op jit(solution)/shard_map/div | solution.py:100
  226.5 8.6 %fusion.22 = f32[1,128,4,2048]{3,2,1,0:T(4,128)} fusion(f32[128,4,2048]{2,1,0:T(4,128)S(1)} %copy-done.4, f32[1,4,2048]{2,1,0:T(4,128)S(1)} %get-tuple-element.25, f32[1,4,2048]{2,1,0:T(4,128)S(1)} %get-tuple-element.24, f32[4,128,4,2048]{3,2,1,0:T(4,128)} %param.3, f32[128]{0:T(128)S(1)} %copy-done.7), kind=kLoop, calls=%fused_computation.61 | loop fusion | flops 10485760 | bytes 16843264 | tf_op jit(solution)/shard_map/stack | solution.py:102
  236.2 23.2 %select_select_fusion = f32[4,130,4,2048]{3,2,1,0:T(4,128)} fusion(f32[4,2,4,2048]{3,2,1,0:T(4,128)S(1)} %broadcast_select_fusion.1, f32[4,2,4,2048]{3,2,1,0:T(4,128)S(1)} %broadcast_select_fusion, f32[4,128,4,2048]{3,2,1,0:T(4,128)} %param.3), kind=kLoop, calls=%fused_computation.11 | loop fusion | flops 55377920 | bytes 34340864 | tf_op jit(solution)/shard_map/jit(_where)/select_n | solution.py:47
  259.4 31.3 %fusion.5 = (f32[4,129,4,2048]{3,2,1,0:T(4,128)S(1)}, f32[4,129,4,2048]{3,2,1,0:T(4,128)}) fusion(f32[4,2,4,2048]{3,2,1,0:T(4,128)S(1)} %broadcast_select_fusion.1, f32[4,130,4,2048]{3,2,1,0:T(4,128)} %select_select_fusion, f32[4,128,4,2048]{3,2,1,0:T(4,128)} %param.3, f32[4,2,4,2048]{3,2,1,0:T(4,128)S(1)} %broadcast_select_fusion), kind=kLoop, calls=%fused_computation.17 | loop fusion | flops 25362432 | bytes 84934656 | tf_op jit(solution)/shard_map/add | solution.py:72
  290.8 14.4 %fusion.48 = (f32[129,4,2048]{2,1,0:T(4,128)}, f32[129,4,2048]{2,1,0:T(4,128)}, f32[129,4,2048]{2,1,0:T(4,128)}, f32[129,4,2048]{2,1,0:T(4,128)}, f32[129,4,2048]{2,1,0:T(4,128)}) fusion(f32[4,129,4,2048]{3,2,1,0:T(4,128)S(1)} %get-tuple-element.6, f32[4,129,4,2048]{3,2,1,0:T(4,128)} %get-tuple-element.7), kind=kLoop, calls=%fused_computation.111 | loop fusion | flops 7397376 | bytes 38043648 | tf_op jit(solution)/shard_map/mul | solution.py:57
  305.8 25.2 %subtract_multiply_fusion = f32[4,129,4,2048]{3,2,1,0:T(4,128)} fusion(f32[4,129,4,2048]{3,2,1,0:T(4,128)} %get-tuple-element.7, f32[4,129,4,2048]{3,2,1,0:T(4,128)} %copy-done.3, f32[129,4,2048]{2,1,0:T(4,128)} %get-tuple-element.10, f32[129,4,2048]{2,1,0:T(4,128)} %get-tuple-element.12, f32[129,4,2048]{2,1,0:T(4,128)} %get-tuple-element.11, ...), kind=kLoop, calls=%fused_computation.20 | loop fusion | flops 50724864 | bytes 71860752 | tf_op jit(solution)/shard_map/mul | solution.py:84
  332.1 39.6 %multiply_add_fusion = f32[4,128,4,2048]{3,2,1,0:T(4,128)} fusion(f32[4,128,4,2048]{3,2,1,0:T(4,128)} %param.3, f32[1,128,4,2048]{3,2,1,0:T(4,128)S(1)} %broadcast.93, f32[1,128,4,2048]{3,2,1,0:T(4,128)} %fusion.21, f32[1,128,4,2048]{3,2,1,0:T(4,128)} %fusion.22, f32[4,128,4,2048]{3,2,1,0:T(4,128)} %multiply_subtract_fusion, ...), kind=kLoop, calls=%fused_computation.30 | loop fusion | flops 58720256 | bytes 113246720 | tf_op jit(solution)/shard_map/add | solution.py:103
  (68 shorter events, 40.2 us)
Async XLA Ops:
  0.6 162.8 %copy-start = (bf16[1,1024,1024]{2,1,0:T(8,128)(2,1)S(1)}, bf16[1,1024,1024]{2,1,0:T(8,128)(2,1)}, u32[]{:S(2)}) copy-start(bf16[1,1024,1024]{2,1,0:T(8,128)(2,1)} %param.4) | copy-start | bytes 6291460
  2.7 232.4 %collective-permute-start.1 = (f32[4,2,4,2048]{3,2,1,0:T(4,128)}, f32[4,2,4,2048]{3,2,1,0:T(4,128)}, u32[]{:S(2)}, u32[]{:S(2)}) collective-permute-start(f32[4,2,4,2048]{3,2,1,0:T(4,128)} %get-tuple-element.19), channel_id=1, source_target_pairs={{4,0},{8,4},{12,8},{16,12},{20,16},{24,20},{28,24},{5,1},{9,5},{13... | collective-permute-start | bytes 786440 | tf_op jit(solution)/shard_map/ppermute | solution.py:25
  4.0 232.2 %collective-permute-start = (f32[4,2,4,2048]{3,2,1,0:T(4,128)}, f32[4,2,4,2048]{3,2,1,0:T(4,128)}, u32[]{:S(2)}, u32[]{:S(2)}) collective-permute-start(f32[4,2,4,2048]{3,2,1,0:T(4,128)} %get-tuple-element.18), channel_id=1, source_target_pairs={{0,4},{4,8},{8,12},{12,16},{16,20},{20,24},{24,28},{1,5},{5,9},{9,... | collective-permute-start | bytes 786440 | tf_op jit(solution)/shard_map/ppermute | solution.py:23
  34.1 128.0 %all-to-all-start = ((bf16[128,4,2,8]{0,1,2,3:T(4,128)(2,1)}), bf16[128,4,2,8]{0,1,2,3:T(4,128)(2,1)S(1)}, u32[]{:S(2)}, u32[]{:S(2)}) async-start(bf16[128,4,2,8]{0,1,2,3:T(4,128)(2,1)} %copy.18), calls=%async_computation | async-start | bytes 32768 | tf_op jit(solution)/shard_map/all_to_all | solution.py:145
  102.6 15.6 %copy-start.6 = (f32[128]{0:T(128)S(1)}, f32[128]{0:T(128)}, u32[]{:S(2)}) copy-start(f32[128]{0:T(128)} %broadcast_add_fusion) | copy-start | bytes 1540
  102.6 17.5 %copy-start.9 = (f32[128]{0:T(128)S(1)}, f32[128]{0:T(128)}, u32[]{:S(2)}) copy-start(f32[128]{0:T(128)} %broadcast_add_fusion.1) | copy-start | bytes 1540
  115.0 18.9 %copy-start.2 = (f32[4,128,4,2047]{3,2,1,0:T(4,128)}, f32[4,128,4,2047]{3,2,1,0:T(4,128)S(1)}, u32[]{:S(2)}) copy-start(f32[4,128,4,2047]{3,2,1,0:T(4,128)S(1)} %slice.206) | copy-start | bytes 50307076
  168.3 12.7 %all-to-all-start.1 = ((f32[8,1,1024]{2,1,0:T(1,128)}), f32[8,1,1024]{2,1,0:T(1,128)S(1)}, u32[]{:S(2)}, u32[]{:S(2)}) async-start(f32[8,1,1024]{2,1,0:T(1,128)} %reshape.122), calls=%async_computation.1 | async-start | bytes 65536 | tf_op jit(solution)/shard_map/all_to_all | solution.py:148
  185.6 27.8 %copy-start.7 = (f32[128]{0:T(128)S(1)}, f32[128]{0:T(128)}, u32[]{:S(2)}) copy-start(f32[128]{0:T(128)} %broadcast_add_fusion) | copy-start | bytes 1540
  189.4 2.0 copy-start.5
  207.0 18.6 %collective-permute-start.2 = (f32[1,4,2048]{2,1,0:T(4,128)S(1)}, f32[1,4,2048]{2,1,0:T(4,128)S(1)}, u32[]{:S(2)}, u32[]{:S(2)}) collective-permute-start(f32[1,4,2048]{2,1,0:T(4,128)S(1)} %get-tuple-element.26), channel_id=1, source_target_pairs={{4,0},{8,4},{12,8},{16,12},{20,16},{24,20},{28,24},{5,1},{9,5},{13... | collective-permute-start | bytes 98312 | tf_op jit(solution)/shard_map/ppermute | solution.py:25
  208.3 17.3 %collective-permute-start.3 = (f32[1,4,2048]{2,1,0:T(4,128)S(1)}, f32[1,4,2048]{2,1,0:T(4,128)S(1)}, u32[]{:S(2)}, u32[]{:S(2)}) collective-permute-start(f32[1,4,2048]{2,1,0:T(4,128)S(1)} %get-tuple-element.27), channel_id=1, source_target_pairs={{0,4},{4,8},{8,12},{12,16},{16,20},{20,24},{24,28},{1,5},{5,9},{9,... | collective-permute-start | bytes 98312 | tf_op jit(solution)/shard_map/ppermute | solution.py:23
  213.4 13.0 %copy-start.4 = (f32[128,4,2048]{2,1,0:T(4,128)S(1)}, f32[128,4,2048]{2,1,0:T(4,128)}, u32[]{:S(2)}) copy-start(f32[128,4,2048]{2,1,0:T(4,128)} %reshape.119) | copy-start | bytes 12582916
  290.8 15.0 %copy-start.3 = (f32[4,129,4,2048]{3,2,1,0:T(4,128)}, f32[4,129,4,2048]{3,2,1,0:T(4,128)S(1)}, u32[]{:S(2)}) copy-start(f32[4,129,4,2048]{3,2,1,0:T(4,128)S(1)} %get-tuple-element.6) | copy-start | bytes 50724868
  290.8 15.0 %copy-start.8 = (f32[129]{0:T(256)S(1)}, f32[129]{0:T(256)}, u32[]{:S(2)}) copy-start(f32[129]{0:T(256)} %pad_maximum_fusion.10) | copy-start | bytes 1552
  290.8 15.0 %copy-start.10 = (f32[4]{0:T(128)S(1)}, f32[4]{0:T(128)}, u32[]{:S(2)}) copy-start(f32[4]{0:T(128)} %compare_convert_fusion.1) | copy-start | bytes 52
  332.1 39.6 %copy-start.1 = (bf16[1,1024,1024]{2,1,0:T(8,128)(2,1)S(1)}, bf16[1,1024,1024]{2,1,0:T(8,128)(2,1)}, u32[]{:S(2)}) copy-start(bf16[1,1024,1024]{2,1,0:T(8,128)(2,1)} %param.4) | copy-start | bytes 6291460
where the time goes:
time: 378 us; the launch traced here: 372 us
  other arithmetic  231 us (61%)
  local copies, waits for them, and re-layouts  91.5 us (24%)
  starting transfers between devices  24.9 us (7%)
  matrix products  11.3 us (3%)
  waiting for transfers between devices  5.89 us (2%)
  blocking collectives  5.57 us (1%)
    add x1, other arithmetic, advance(): return interior + step_time * (tendency + sources)  39.6 us
    add x1, other arithmetic, advance(): centre_cells[:, :-1] + 0.5 * slopes[:, :-1]  31.3 us
    slice x2, local copies, waits for them, and re-layouts, advance(): jnp.roll(interior, 1, axis=3)  30.5 us
    sub x1, other arithmetic, advance(): interior - 0.5 * phi_slopes  29.8 us
    sub x1, other arithmetic, rusanov(): 0.5 * (flux_left + flux_right) - 0.5 * reach * (right_state - left_state)  25.8 us
    mul x1, other arithmetic, advance(): weighted = face_radii * flux_radial  25.2 us
    select_n x1, other arithmetic, minmod(): jnp.where(former * latter > 0, jnp.where(jnp.abs(former) < jnp.abs(latter...  23.2 us
    slice x2, local copies, waits for them, and re-layouts, advance(): jnp.roll(interior - 0.5 * phi_slopes, -1, axis=3)  14.5 us
  transfers between devices with their start and end apart: 6, of which 1 were waited for; matrix products, arithmetic and copies ran while one was open for 52% of the time, Pallas kernels for 0%

commit v1 on v0

--- a/solution.py
+++ b/solution.py
@@ -2,7 +2,10 @@
 
 import jax
 import jax.numpy as jnp
+import numpy as np
 from jax import lax
+from jax.experimental import pallas as pl
+from jax.experimental.pallas import tpu as pltpu
 from jax.sharding import PartitionSpec as P
 
 sound_sq = 1.0
@@ -121,7 +124,7 @@
     return jnp.concatenate([low_rim, middle, high_rim], axis=axis_dim)
 
 
-def body(state, green, vertical):
+def plain_body(state, green, vertical):
     radii, planes, azimuth = (state.shape[1], state.shape[2], state.shape[3])
     modes_dev, radial_all = (green.shape[0], green.shape[1])
     modes = modes_dev * lax.axis_size("row")
@@ -162,6 +165,657 @@
     return (new_state, potential)
 
 
+LANES = 128
+SUBS = 8
+HALF = 4
+PAIRS = ((0, 0), (0, 1), (1, 0), (0, 2), (2, 0), (1, 1))
+
+
+def np_split3(values):
+    high = np.asarray(values, np.float32)
+    parts = []
+    for _ in range(3):
+        part = high.astype(jnp.bfloat16)
+        parts.append(part)
+        high = high - part.astype(np.float32)
+    return parts
+
+
+def np_tables(azimuth, modes):
+    index = np.arange(azimuth)[:, None] * np.arange(modes)[None, :] % azimuth
+    angles = index * (2.0 * np.pi / azimuth)
+    forward = np.concatenate([np.cos(angles), -np.sin(angles)], axis=1)
+    weights = np.where(np.arange(modes) == 0, 1.0, 2.0) / azimuth
+    inverse = forward.T * np.concatenate([weights, weights])[:, None]
+    phi_step = 2.0 * np.pi / azimuth
+    turned = (np.roll(inverse, -1, 1) - np.roll(inverse, 1, 1)) / (2.0 * phi_step)
+    return (forward, inverse, turned)
+
+
+def forward_table(forward):
+    azimuth, width = forward.shape
+    tiles = azimuth // (2 * LANES)
+    table = np.zeros((tiles, LANES, 2, HALF, width), jnp.bfloat16)
+    blocks = forward.reshape(tiles, 2, LANES, width)
+    for q, part in enumerate(np_split3(blocks)):
+        table[:, :, :, q] = part.transpose(0, 2, 1, 3)
+    return table.reshape(tiles * LANES, 2 * HALF * width)
+
+
+def inverse_table(inverse):
+    width, azimuth = inverse.shape
+    tiles = azimuth // (2 * LANES)
+    parts = np_split3(inverse.reshape(width, tiles, 2, LANES))
+    table = np.zeros((2, LANES // width, width, tiles, LANES), jnp.bfloat16)
+    for q, (_, right) in enumerate(PAIRS):
+        table[:, q] = parts[right].transpose(2, 0, 1, 3)
+    return table.reshape(2 * LANES, tiles * LANES)
+
+
+def split3(values):
+    parts = []
+    for _ in range(3):
+        part = values.astype(jnp.bfloat16)
+        parts.append(part)
+        values = values - part.astype(jnp.float32)
+    return parts
+
+
+def lane_of(shape):
+    return lax.broadcasted_iota(jnp.int32, shape, len(shape) - 1)
+
+
+def spectrum_kernel(copies, cells_ref, table_ref, out_ref, sums_ref):
+    step = pl.program_id(0)
+    rows, _, _ = cells_ref.shape[1:]
+    tiles = cells_ref.shape[2] // SUBS
+    total = None
+    for t in range(0, tiles, 2):
+        cells = jnp.concatenate(
+            [
+                cells_ref[0, :, (t + h) * SUBS : (t + h + 1) * SUBS, :].reshape(rows * SUBS, LANES)
+                for h in range(2)
+            ],
+            axis=1,
+        )
+        table = table_ref[t * LANES : (t + 2) * LANES, :]
+        for part in split3(cells):
+            term = jnp.dot(part, table, preferred_element_type=jnp.float32)
+            total = term if total is None else total + term
+    sums_ref[pl.ds(pl.multiple_of(step * rows * SUBS, SUBS), rows * SUBS), :] = total
+
+    @pl.when(step == pl.num_programs(0) - 1)
+    def _():
+        radii = sums_ref.shape[0] // SUBS
+        modes = out_ref.shape[0]
+        width = 2 * modes
+        lane = lane_of((radii, LANES))
+        for z in range(HALF):
+            former = sums_ref[pl.ds(z, radii, stride=SUBS), :]
+            latter = sums_ref[pl.ds(HALF + z, radii, stride=SUBS), :]
+            turned = jnp.where(lane < LANES // 2, former, latter).T
+            both = turned[: LANES // 2] + turned[LANES // 2 :]
+            value = both[:width] + both[width : 2 * width] + both[2 * width : 3 * width]
+            for c in range(2):
+                for g in range(copies):
+                    out_ref[:, g, c * HALF + z, :] = value[c * modes : (c + 1) * modes]
+
+
+def green_kernel(cells_ref, weights_ref, green_ref, out_ref):
+    blocks = cells_ref.shape[0]
+    mixed = [
+        jnp.dot(
+            weights_ref[...],
+            cells_ref[i],
+            precision=precise,
+            preferred_element_type=jnp.float32,
+        )
+        for i in range(blocks)
+    ]
+    mixed = jnp.concatenate(mixed, axis=1).astype(jnp.bfloat16)
+    pot = lax.dot_general(
+        mixed, green_ref[0], (((1,), (1,)), ((), ())), preferred_element_type=jnp.float32
+    )
+    lane = lane_of((SUBS, LANES))
+    pieces = [pot[:, i * LANES : (i + 1) * LANES] for i in range(blocks)]
+    for i in range(blocks):
+        out_ref[i, 0] = pieces[i]
+        low = pieces[0] if i == 0 else pltpu.roll(pieces[i - 1], 1, 1)
+        if i == blocks - 1:
+            high = pltpu.roll(pieces[i], 2, 1)
+        else:
+            high = pltpu.roll(pieces[i + 1], 1, 1)
+        out_ref[i, 1] = jnp.where(lane == 0, low, high)
+
+
+def limited(former, latter):
+    return jnp.maximum(jnp.minimum(former, latter), jnp.minimum(jnp.maximum(former, latter), 0.0))
+
+
+def face_flux(left, right, normal):
+    inverse = 1.0 / (left[0] * right[0])
+    speed_left = left[normal] * (right[0] * inverse)
+    speed_right = right[normal] * (left[0] * inverse)
+    reach = jnp.maximum(jnp.abs(speed_left), jnp.abs(speed_right)) + math.sqrt(sound_sq)
+    weight_left = speed_left + reach
+    weight_right = speed_right - reach
+    fluxes = [a * weight_left + b * weight_right for a, b in zip(left, right)]
+    fluxes[normal] = fluxes[normal] + sound_sq * (left[0] + right[0])
+    return fluxes
+
+
+def block_step(cell, base_row, constants, scratch, store, pull, fresh):
+    rows, subs, radial_step, phi_step, step_time = constants
+    d_ref, r_ref, g_ref, w_ref, l_ref, f_ref = scratch
+    tiles = subs // SUBS
+    lane = lane_of((SUBS, LANES))
+    first = lane == 0
+    last = lane == LANES - 1
+
+    def up(here, there):
+        return pltpu.roll(jnp.where(first, there, here), LANES - 1, 1)
+
+    def down(here, there):
+        return pltpu.roll(jnp.where(last, there, here), 1, 1)
+
+    def span(k, shift):
+        return pl.ds(k * SUBS + SUBS + shift, SUBS)
+
+    def radial_face(r, k):
+        part = pl.ds(k * SUBS, SUBS)
+        left, right = [], []
+        for f in range(4):
+            here, above, far = cell(f, r, k), cell(f, r + 1, k), cell(f, r + 2, k)
+            slope = limited(above - here, far - above)
+            twice = above + above
+            left.append(l_ref[f, part, :])
+            right.append(twice - slope)
+            l_ref[f, part, :] = twice + slope
+        return face_flux(left, right, 1)
+
+    @pl.when(fresh)
+    def _():
+        for k in range(tiles):
+            part = pl.ds(k * SUBS, SUBS)
+            for f in range(4):
+                lower, here, above = cell(f, -2, k), cell(f, -1, k), cell(f, 0, k)
+                l_ref[f, part, :] = (here + here) + limited(here - lower, above - here)
+            for f, value in enumerate(radial_face(-1, k)):
+                f_ref[f, part, :] = value
+
+    for r in range(rows):
+        slot = r % 2
+        index = (base_row + r).astype(jnp.float32)
+        centre = inner_radius + (jnp.full((SUBS, LANES), index, jnp.float32) + 0.5) * radial_step
+        over = step_time / centre
+        scale = over * (0.25 / radial_step)
+        outer = scale * (centre + 0.5 * radial_step)
+        inner = scale * (centre - 0.5 * radial_step)
+        turn = over * (0.25 / phi_step)
+        for k in range(tiles):
+            for f in range(4):
+                here = cell(f, r, k)
+                if k + 1 < tiles:
+                    there = cell(f, r, k, HALF)
+                else:
+                    there = jnp.concatenate(
+                        [cell(f, r, k)[HALF:], cell(f, r, 0)[:HALF]], axis=0
+                    )
+                delta = up(here, there) - here
+                d_ref[slot, f, span(k, 0), :] = delta
+                if k == tiles - 1:
+                    d_ref[slot, f, HALF:SUBS, :] = delta[HALF:]
+        for k in range(tiles):
+            for f in range(4):
+                here = cell(f, r, k)
+                ahead = d_ref[slot, f, span(k, 0), :]
+                behind = down(ahead, d_ref[slot, f, span(k, -HALF), :])
+                slope = limited(behind, ahead)
+                twice = here + here
+                w_ref[slot, f, span(k, 0), :] = twice + slope
+                right = twice - slope
+                r_ref[slot, f, span(k, 0), :] = right
+                if k == 0:
+                    r_ref[slot, f, pl.ds(SUBS + subs, HALF), :] = right[:HALF]
+        for k in range(tiles):
+            left = [w_ref[slot, f, span(k, 0), :] for f in range(4)]
+            right = [
+                up(r_ref[slot, f, span(k, 0), :], r_ref[slot, f, span(k, HALF), :])
+                for f in range(4)
+            ]
+            for f, value in enumerate(face_flux(left, right, 2)):
+                g_ref[slot, f, span(k, 0), :] = value
+                if k == tiles - 1:
+                    g_ref[slot, f, HALF:SUBS, :] = value[HALF:]
+        for k in range(tiles):
+            part = pl.ds(k * SUBS, SUBS)
+            radial = radial_face(r, k)
+            values = [cell(f, r, k) for f in range(4)]
+            density, push, swing, _ = values
+            spin = swing / density
+            extra = [None, (swing * spin + sound_sq * density) * over, (push * spin) * -over, None]
+            for f, value in enumerate(values):
+                flux = g_ref[slot, f, span(k, 0), :]
+                before = down(flux, g_ref[slot, f, span(k, -HALF), :])
+                value = value + (inner * f_ref[f, part, :] - outer * radial[f])
+                value = value - turn * (flux - before)
+                if extra[f] is not None:
+                    value = value + extra[f]
+                    if pull is not None:
+                        value = value - density * pull(f - 1, r, k)
+                f_ref[f, part, :] = radial[f]
+                store(f, r, k, value)
+
+
+def spectral_rows(modes_ref, left_ref, radial_step, step_time):
+    modes = modes_ref.shape[0]
+    width = 2 * modes
+    radii = LANES
+    lane = lane_of((modes, LANES))
+    index = (lane + lax.axis_index("row") * radii).astype(jnp.float32)
+    over = step_time / (inner_radius + (index + 0.5) * radial_step)
+    left_ref[...] = jnp.zeros_like(left_ref)
+    for z in range(HALF):
+        kinds = ([], [], [])
+        for c in range(2):
+            here = modes_ref[:, 0, c * HALF + z, :]
+            edge = modes_ref[:, 1, c * HALF + z, :]
+            above = jnp.where(
+                lane == LANES - 1, pltpu.roll(edge, LANES - 2, 1), pltpu.roll(here, LANES - 1, 1)
+            )
+            below = jnp.where(lane == 0, edge, pltpu.roll(here, 1, 1))
+            kinds[0].append(here)
+            kinds[1].append((above - below) * (step_time / (2.0 * radial_step)))
+            kinds[2].append(here * over)
+        for kind, halves in enumerate(kinds):
+            parts = [part.astype(jnp.float32) for part in split3(jnp.concatenate(halves, axis=0))]
+            stack = [parts[left] for left, _ in PAIRS]
+            stack += [jnp.zeros((LANES - len(PAIRS) * width, LANES), jnp.float32)]
+            turned = jnp.concatenate(stack, axis=0).T
+            for p in range(2):
+                left_ref[kind, p, pl.ds(p * HALF + z, radii, stride=SUBS), :] = turned
+
+
+def muscl_kernel(plan, final, *refs):
+    rows, subs, radii, radial_all, start, count, done = plan
+    if final:
+        cells, low, high, modes_ref, pot_table, turn_table, old, out, pot_out, *refs = refs
+        left_ref, pull_ref, pot_buf, late_buf, pot_sem, late_sem, *refs = refs
+    else:
+        cells, out, *refs = refs
+    in_buf, out_buf, in_sem, out_sem, *scratch = refs
+    azimuth = subs // HALF * LANES
+    phi_step = 2.0 * math.pi / azimuth
+    radial_step = radial_span / radial_all
+    step_time = courant * min(radial_step, inner_radius * phi_step)
+    blocks = radii // rows
+    size = rows * subs
+    full = (rows + 4) * subs
+    position = lax.axis_index("row")
+    last_rank = lax.axis_size("row") - 1
+    tiles = subs // SUBS
+
+    def place(n):
+        return lax.rem(start + n, blocks)
+
+    def copy_in(source, f, first, length, slot, offset):
+        return pltpu.make_async_copy(
+            source.at[f, pl.ds(first, length), :],
+            in_buf.at[slot, f, pl.ds(offset, length), :],
+            in_sem.at[slot],
+        )
+
+    def fetch(n, slot):
+        b = place(n)
+        base = pl.multiple_of(b * size, size)
+        inside = (b > 0) & (b < blocks - 1)
+
+        @pl.when(inside)
+        def _():
+            for f in range(4):
+                copy_in(cells, f, base - 2 * subs, full, slot, 0).start()
+
+        if not final:
+            return
+
+        @pl.when(b == 0)
+        def _():
+            for f in range(4):
+                copy_in(cells, f, 0, size + 2 * subs, slot, 2 * subs).start()
+
+            @pl.when(position == 0)
+            def _():
+                for f in range(4):
+                    for h in range(2):
+                        copy_in(cells, f, 0, subs, slot, h * subs).start()
+
+            @pl.when(position != 0)
+            def _():
+                for f in range(4):
+                    copy_in(low, f, 0, 2 * subs, slot, 0).start()
+
+        @pl.when(b == blocks - 1)
+        def _():
+            for f in range(4):
+                copy_in(cells, f, (radii - rows - 2) * subs, size + 2 * subs, slot, 0).start()
+
+            @pl.when(position == last_rank)
+            def _():
+                for f in range(4):
+                    for h in range(2):
+                        copy_in(
+                            cells, f, (radii - 1) * subs, subs, slot, size + (2 + h) * subs
+                        ).start()
+
+            @pl.when(position != last_rank)
+            def _():
+                for f in range(4):
+                    copy_in(high, f, 0, 2 * subs, slot, size + 2 * subs).start()
+
+    def arrived(slot):
+        for f in range(4):
+            copy_in(cells, f, 0, full, slot, 0).wait()
+
+    def give(n, slot):
+        base = pl.multiple_of(place(n) * size, size)
+        copies = [
+            pltpu.make_async_copy(
+                out_buf.at[slot, f, pl.ds(0, size), :],
+                out.at[f, pl.ds(base, size), :],
+                out_sem.at[slot],
+            )
+            for f in range(4)
+        ]
+        if final:
+            copies.append(
+                pltpu.make_async_copy(
+                    pot_buf.at[slot], pot_out.at[pl.ds(base, size), :], out_sem.at[slot]
+                )
+            )
+        return copies
+
+    fetch(0, 0)
+    if final:
+        spectral_rows(modes_ref, left_ref, radial_step, step_time)
+
+    def spectral(b, pot_slot):
+        span = pl.ds(pl.multiple_of(b * rows * SUBS, SUBS), rows * SUBS)
+
+        def product(kinds, table):
+            left = [
+                jnp.concatenate([left_ref[kind, p, span, :] for p in range(2)], axis=1)
+                for kind in kinds
+            ]
+            left = jnp.concatenate(left, axis=0).astype(jnp.bfloat16)
+            return jnp.dot(left, table[...], preferred_element_type=jnp.float32)
+
+        both = product((0, 1), pot_table)
+        turn = product((2,), turn_table)
+        for r in range(rows):
+            for t in range(tiles):
+                part = pl.ds(r * subs + t * SUBS, SUBS)
+                column = slice(t * LANES, (t + 1) * LANES)
+                line = slice(r * SUBS, (r + 1) * SUBS)
+                pot_buf[pot_slot, part, :] = both[line, column]
+                pull_ref[0, part, :] = both[rows * SUBS + r * SUBS : rows * SUBS + (r + 1) * SUBS, column]
+                pull_ref[1, part, :] = turn[line, column]
+
+    def body(n, carry):
+        slot = lax.rem(n, 2)
+
+        @pl.when(n + 1 < count)
+        def _():
+            fetch(n + 1, 1 - slot)
+
+        @pl.when(n >= 2)
+        def _():
+            for copy in give(n - 2, slot):
+                copy.wait()
+
+        b = place(n)
+        pull = None
+        if final:
+            spectral(b, slot)
+
+            def pull(kind, r, k):
+                return pull_ref[kind, pl.ds(r * subs + k * SUBS, SUBS), :]
+
+        arrived(slot)
+
+        def cell(f, r, k, shift=0):
+            return in_buf[slot, f, pl.ds((r + 2) * subs + k * SUBS + shift, SUBS), :]
+
+        def store(f, r, k, value):
+            out_buf[slot, f, pl.ds(r * subs + k * SUBS, SUBS), :] = value
+
+        constants = (rows, subs, radial_step, phi_step, step_time)
+        block_step(
+            cell, position * radii + b * rows, constants, scratch, store, pull, (n == 0) | (b == 0)
+        )
+        for copy in give(n, slot):
+            copy.start()
+        return carry
+
+    lax.fori_loop(0, count, body, 0)
+    for n in range(max(count - 2, 0), count):
+        for copy in give(n, n % 2):
+            copy.wait()
+    if not final:
+        return
+
+    def late_in(n, slot):
+        base = pl.multiple_of((1 + n) * size, size)
+        return [
+            pltpu.make_async_copy(
+                source.at[f, pl.ds(base, size), :], late_buf.at[slot, i], late_sem.at[slot]
+            )
+            for i, (source, f) in enumerate(((cells, 0), (out, 1), (out, 2)))
+        ]
+
+    def late_out(n, slot):
+        base = pl.multiple_of((1 + n) * size, size)
+        copies = [
+            pltpu.make_async_copy(
+                out_buf.at[slot, f, pl.ds(0, size), :],
+                out.at[f, pl.ds(base, size), :],
+                pot_sem.at[slot],
+            )
+            for f in (1, 2)
+        ]
+        copies.append(
+            pltpu.make_async_copy(
+                pot_buf.at[slot], pot_out.at[pl.ds(base, size), :], pot_sem.at[slot]
+            )
+        )
+        return copies
+
+    for copy in late_in(0, 0):
+        copy.start()
+
+    def late(n, carry):
+        slot = lax.rem(n, 2)
+
+        @pl.when(n + 1 < done)
+        def _():
+            for copy in late_in(n + 1, 1 - slot):
+                copy.start()
+
+        @pl.when(n >= 2)
+        def _():
+            for copy in late_out(n - 2, slot):
+                copy.wait()
+
+        spectral(1 + n, slot)
+        for copy in late_in(n, slot):
+            copy.wait()
+        for t in range(rows * tiles):
+            part = pl.ds(t * SUBS, SUBS)
+            density = late_buf[slot, 0, part, :]
+            for f in (1, 2):
+                out_buf[slot, f, part, :] = (
+                    late_buf[slot, f, part, :] - density * pull_ref[f - 1, part, :]
+                )
+        for copy in late_out(n, slot):
+            copy.start()
+        return carry
+
+    lax.fori_loop(0, done, late, 0)
+    for n in range(max(done - 2, 0), done):
+        for copy in late_out(n, n % 2):
+            copy.wait()
+
+
+def vmem_limit(mebibytes):
+    return pltpu.CompilerParams(vmem_limit_bytes=mebibytes * 2**20)
+
+
+def muscl(operands, plan, final, shape):
+    rows, subs, radii, _, _, count, _ = plan
+    fields = shape[0]
+    size = rows * subs
+    pad = subs + 3 * SUBS
+    anywhere = pl.BlockSpec(memory_space=pl.ANY)
+    whole = pl.BlockSpec(memory_space=pltpu.VMEM)
+    carried = [
+        pltpu.VMEM((2, fields, (rows + 4) * subs + SUBS, LANES), jnp.float32),
+        pltpu.VMEM((2, fields, size + SUBS, LANES), jnp.float32),
+        pltpu.SemaphoreType.DMA((2,)),
+        pltpu.SemaphoreType.DMA((2,)),
+    ]
+    carried += [pltpu.VMEM((2, fields, pad, LANES), jnp.float32) for _ in range(4)]
+    carried += [pltpu.VMEM((fields, subs + SUBS, LANES), jnp.float32) for _ in range(2)]
+    out_shape = [jax.ShapeDtypeStruct(shape, jnp.float32)]
+    if final:
+        in_specs = [anywhere] * 3 + [whole] * 3 + [anywhere]
+        out_shape.append(jax.ShapeDtypeStruct(shape[1:], jnp.float32))
+        aliases = {6: 0}
+        carried = [
+            pltpu.VMEM((3, 2, radii * SUBS, LANES), jnp.float32),
+            pltpu.VMEM((2, size, LANES), jnp.float32),
+            pltpu.VMEM((2, size, LANES), jnp.float32),
+            pltpu.VMEM((2, 3, size, LANES), jnp.float32),
+            pltpu.SemaphoreType.DMA((2,)),
+            pltpu.SemaphoreType.DMA((2,)),
+        ] + carried
+    else:
+        in_specs = [anywhere]
+        aliases = {}
+    return pl.pallas_call(
+        lambda *refs: muscl_kernel(plan, final, *refs),
+        name="muscl_final" if final else "muscl_early",
+        in_specs=in_specs,
+        out_specs=[anywhere] * len(out_shape),
+        out_shape=out_shape,
+        input_output_aliases=aliases,
+        scratch_shapes=carried,
+        compiler_params=vmem_limit(50),
+        cost_estimate=pl.CostEstimate(
+            flops=count * rows * subs * LANES * 1500,
+            bytes_accessed=count * size * LANES * 32,
+            transcendentals=0,
+        ),
+    )(*operands)
+
+
+def fast_body(state, green, vertical):
+    fields, radii, planes, azimuth = state.shape
+    radial_all = green.shape[1]
+    ranks, stacks = lax.axis_size("row"), lax.axis_size("gz")
+    modes = green.shape[0] * ranks
+    subs = azimuth // LANES * planes
+    forward, inverse, turned = np_tables(azimuth, modes)
+    cells = (
+        state.reshape(fields, radii, planes, azimuth // LANES, LANES)
+        .transpose(0, 1, 3, 2, 4)
+        .reshape(fields, radii, subs, LANES)
+    )
+    up_ring = [(i, i + 1) for i in range(ranks - 1)]
+    low = lax.ppermute(cells[:, radii - 2 :], "row", up_ring)
+    high = lax.ppermute(cells[:, :2], "row", [(j, i) for i, j in up_ring])
+
+    rows = 16
+    spectrum = pl.pallas_call(
+        lambda *refs: spectrum_kernel(stacks, *refs),
+        name="spectrum",
+        grid=(radii // rows,),
+        in_specs=[
+            pl.BlockSpec((1, rows, subs, LANES), lambda i: (0, i, 0, 0)),
+            pl.BlockSpec((azimuth // 2, LANES), lambda i: (0, 0)),
+        ],
+        out_specs=pl.BlockSpec((modes, stacks, SUBS, LANES), lambda i: (0, 0, 0, 0)),
+        out_shape=jax.ShapeDtypeStruct((modes, stacks, SUBS, LANES), jnp.float32),
+        scratch_shapes=[pltpu.VMEM((radii * SUBS, LANES), jnp.float32)],
+        compiler_params=vmem_limit(54),
+        cost_estimate=pl.CostEstimate(flops=2**33, bytes_accessed=2**22, transcendentals=0),
+    )(cells, forward_table(forward))
+
+    gathered = lax.all_to_all(
+        spectrum.reshape(ranks * stacks, SUBS, LANES), ("row", "gz"), 0, 0, tiled=True
+    )
+    own = lax.dynamic_slice_in_dim(vertical, lax.axis_index("gz") * planes, planes, 0)
+    own = own.reshape(planes, stacks, planes)
+    weights = jnp.einsum("cd,zgy->czgdy", jnp.eye(2, dtype=jnp.float32), own, precision=precise)
+    weights = weights.reshape(SUBS, stacks * SUBS)
+
+    pot_modes = pl.pallas_call(
+        green_kernel,
+        name="green",
+        in_specs=[pl.BlockSpec(memory_space=pltpu.VMEM)] * 3,
+        out_specs=pl.BlockSpec(memory_space=pltpu.VMEM),
+        out_shape=jax.ShapeDtypeStruct((ranks, 2, SUBS, LANES), jnp.float32),
+        compiler_params=vmem_limit(16),
+        cost_estimate=pl.CostEstimate(flops=2**30, bytes_accessed=2**21, transcendentals=0),
+    )(gathered.reshape(ranks, stacks * SUBS, LANES), weights, green)
+    pot_spec = lax.all_to_all(pot_modes, "row", 0, 0, tiled=True)
+
+    rows, early = 8, 3
+    blocks = radii // rows
+    flat = cells.reshape(fields, radii * subs, LANES)
+    flat_low = low.reshape(fields, 2 * subs, LANES)
+    flat_high = high.reshape(fields, 2 * subs, LANES)
+    plan = (rows, subs, radii, radial_all, 1, early, 0)
+    (partial,) = muscl([flat], plan, False, flat.shape)
+    plan = (rows, subs, radii, radial_all, 1 + early, blocks - early, early)
+    new_cells, potential = muscl(
+        [
+            flat,
+            flat_low,
+            flat_high,
+            pot_spec,
+            inverse_table(inverse),
+            inverse_table(turned),
+            partial,
+        ],
+        plan,
+        True,
+        flat.shape,
+    )
+    new_state = (
+        new_cells.reshape(fields, radii, azimuth // LANES, planes, LANES)
+        .transpose(0, 1, 3, 2, 4)
+        .reshape(state.shape)
+    )
+    potential = (
+        potential.reshape(radii, azimuth // LANES, planes, LANES)
+        .transpose(0, 2, 1, 3)
+        .reshape(state.shape[1:])
+    )
+    return (new_state, potential)
+
+
+def body(state, green, vertical):
+    _, radii, planes, azimuth = state.shape
+    modes = green.shape[0] * lax.axis_size("row")
+    fits = (
+        planes == HALF
+        and azimuth % (4 * LANES) == 0
+        and radii == LANES
+        and green.shape[0] == 1
+        and modes == SUBS
+    )
+    return (fast_body if fits else plain_body)(state, green, vertical)
+
+
 def solution(mesh):
     placed = (P(None, "row", "gz", None), P("row", None, None), P())
     return jax.shard_map(

time: 378 us -> 88.6 us (0.23); the launches traced: 372 us -> 88.1 us
  other arithmetic: 231 us -> 0.09 us
  local copies, waits for them, and re-layouts: 91.5 us -> 2.88 us
  Pallas kernels: 0 us -> 65.5 us
  matrix products: 11.3 us -> 0 us
  starting transfers between devices: 24.9 us -> 18 us
  blocking collectives: 5.57 us -> 0 us
  waiting for transfers between devices: 5.89 us -> 0.95 us
    add x3 -> x0, other arithmetic: 71.5 us -> none  [the longest x1 39.6 us: advance(): return interior + step_time * (tendency + sources)]
    pallas_call x0 -> x4, Pallas kernels: none -> 65.5 us  [the longest x2 56.9 us: muscl(): pl.pallas_call(lambda *refs: muscl_kernel(plan, final, *refs), name='musc...]
    sub x3 -> x0, other arithmetic: 56.1 us -> none  [the longest x1 29.8 us: advance(): interior - 0.5 * phi_slopes]
    slice x12 -> x1, local copies, waits for them, and re-layouts: 56.3 us -> 1.08 us  [fast_body(): high = lax.ppermute(cells[:, :2], 'row', [(j, i) for i, j in up_ring])]
    mul x3 -> x0, other arithmetic: 52.4 us -> none  [the longest x1 25.2 us: advance(): weighted = face_radii * flux_radial]
    select_n x4 -> x0, other arithmetic: 25.2 us -> none  [the longest x1 23.2 us: minmod(): jnp.where(former * latter > 0, jnp.where(jnp.abs(former) < jnp.abs(latter...]
    div x2 -> x0, other arithmetic: 12.6 us -> none  [the longest x1 12.1 us: advance(): force_phi = -(interior[1] * spin + density * azimuth_slope) / radius_cells]
    dot_general x4 -> x0, matrix products: 11.3 us -> none  [the longest x1 5.66 us: body(): jnp.dot(state[0].reshape(-1, azimuth), forward, precision=precise, prefer...]
  transfers between devices with their start and end apart: 6 -> 4, of which waited for: 1 -> 1; matrix products, arithmetic and copies ran while one was open for 52% -> 2% of each run, Pallas kernels for 0% -> 14%
where the time goes in v1:
time: 88.6 us; the launch traced here: 88.1 us
  Pallas kernels  65.5 us (74%)
  starting transfers between devices  18 us (20%)
  local copies, waits for them, and re-layouts  2.88 us (3%)
  waiting for transfers between devices  0.95 us (1%)
    pallas_call x2, Pallas kernels, muscl(): pl.pallas_call(lambda *refs: muscl_kernel(plan, final, *refs), name='musc...  56.9 us
    all_to_all x1, starting transfers between devices, fast_body(): lax.all_to_all(spectrum.reshape(ranks * stacks, SUBS, LANES), ('row', 'gz...  7.3 us
    pallas_call x1, Pallas kernels, fast_body(): pl.pallas_call(lambda *refs: spectrum_kernel(stacks, *refs), name='spectr...  7.06 us
    all_to_all x1, starting transfers between devices, fast_body(): pot_spec = lax.all_to_all(pot_modes, 'row', 0, 0, tiled=True)  4.81 us
    ppermute x1, starting transfers between devices, fast_body(): low = lax.ppermute(cells[:, radii - 2:], 'row', up_ring)  4.56 us
  transfers between devices with their start and end apart: 4, of which 1 were waited for; matrix products, arithmetic and copies ran while one was open for 2% of the time, Pallas kernels for 14%

profile of v1, /device:TPU:0, one launch (start us, length us, event | category | flops | bytes accessed | tf_op | source)
XLA Modules:
  0.0 88.1 jit_solution(18002864126033469814)
XLA Ops:
  0.6 0.0 copy-start
  0.6 7.1 %spectrum.1 = f32[8,4,8,128]{3,2,1,0:T(8,128)} custom-call(f32[4,128,64,128]{3,2,1,0:T(8,128)} %bitcast.26, bf16[1024,128]{1,0:T(8,128)(2,1)} %constant.16.clone.refs_1_), custom_call_target="tpu_custom_call" | custom-call | flops 8589934592 | bytes 4194304 | tf_op jit(solution)/shard_map/spectrum/pallas_call | solution.py:737
  7.7 7.3 %all-to-all-start = ((f32[32,8,128]{2,1,0:T(8,128)}), f32[32,8,128]{2,1,0:T(8,128)S(1)}, u32[]{:S(2)}, u32[]{:S(2)}) async-start(f32[32,8,128]{2,1,0:T(8,128)} %bitcast.31), calls=%async_computation | async-start | bytes 262144 | tf_op jit(solution)/shard_map/all_to_all | solution.py:752
  15.0 1.1 %fusion = (f32[4,2,64,128]{3,2,1,0:T(8,128)S(1)}, f32[4,2,64,128]{3,2,1,0:T(8,128)S(1)}) fusion(f32[4,128,64,128]{3,2,1,0:T(8,128)} %bitcast.27), kind=kLoop, calls=%fused_computation.3 | loop fusion | bytes 1048576 | tf_op jit(solution)/shard_map/slice | solution.py:734
  16.1 1.3 %collective-permute-start.1 = (f32[4,2,64,128]{3,2,1,0:T(8,128)S(1)}, f32[4,2,64,128]{3,2,1,0:T(8,128)S(1)}, u32[]{:S(2)}, u32[]{:S(2)}) collective-permute-start(f32[4,2,64,128]{3,2,1,0:T(8,128)S(1)} %get-tuple-element.6), channel_id=1, source_target_pairs={{4,0},{8,4},{12,8},{16,12},{20,16},{24,20},{28,24},{5,1},{9,5},{13... | collective-permute-start | bytes 786440 | tf_op jit(solution)/shard_map/ppermute | solution.py:734
  17.4 4.6 %collective-permute-start = (f32[4,2,64,128]{3,2,1,0:T(8,128)S(1)}, f32[4,2,64,128]{3,2,1,0:T(8,128)S(1)}, u32[]{:S(2)}, u32[]{:S(2)}) collective-permute-start(f32[4,2,64,128]{3,2,1,0:T(8,128)S(1)} %get-tuple-element.7), channel_id=1, source_target_pairs={{0,4},{4,8},{8,12},{12,16},{16,20},{20,24},{24,28},{1,5},{5,9},{9,... | collective-permute-start | bytes 786440 | tf_op jit(solution)/shard_map/ppermute | solution.py:733
  22.0 0.0 copy-done
  22.0 0.1 reshape.46
  22.1 0.1 multiply_bitcast_fusion
  22.2 0.1 reshape.47.weights_ref
  22.3 0.9 %all-to-all-done = f32[32,8,128]{2,1,0:T(8,128)S(1)} async-done(((f32[32,8,128]{2,1,0:T(8,128)}), f32[32,8,128]{2,1,0:T(8,128)S(1)}, u32[]{:S(2)}, u32[]{:S(2)}) %all-to-all-start) | async-done | bytes 131104 | tf_op jit(solution)/shard_map/all_to_all | solution.py:752
  23.2 0.0 copy-start.3
  23.2 1.6 %copy-done.3 = bf16[1,1024,1024]{2,1,0:T(8,128)(2,1)S(1)} copy-done((bf16[1,1024,1024]{2,1,0:T(8,128)(2,1)S(1)}, bf16[1,1024,1024]{2,1,0:T(8,128)(2,1)}, u32[]{:S(2)}) %copy-start.3) | copy-done | bytes 2097176
  24.8 1.5 %green.1 = f32[8,2,8,128]{3,2,1,0:T(8,128)} custom-call(f32[8,32,128]{2,1,0:T(8,128)S(1)} %bitcast.25, f32[8,32]{1,0:T(8,128)S(1)} %reshape.47.weights_ref, bf16[1,1024,1024]{2,1,0:T(8,128)(2,1)S(1)} %copy-done.3), custom_call_target="tpu_custom_call" | custom-call | flops 1073741824 | bytes 2097152 | tf_op jit(solution)/shard_map/green/pallas_call | solution.py:760
  26.3 4.8 %all-to-all-start.1 = ((f32[8,2,8,128]{3,2,1,0:T(8,128)}), f32[8,2,8,128]{3,2,1,0:T(8,128)S(1)}, u32[]{:S(2)}, u32[]{:S(2)}) async-start(f32[8,2,8,128]{3,2,1,0:T(8,128)} %green.1), calls=%async_computation.1 | async-start | bytes 131072 | tf_op jit(solution)/shard_map/all_to_all | solution.py:769
  31.1 0.0 copy-start.1
  31.1 0.0 copy-start.2
  31.1 10.7 %muscl_early.1.refs_6_ = f32[4,8192,128]{2,1,0:T(8,128)} custom-call(f32[4,8192,128]{2,1,0:T(8,128)} %bitcast.28), custom_call_target="tpu_custom_call" | custom-call | flops 294912000 | bytes 6291456 | tf_op jit(solution)/shard_map/muscl_early/pallas_call | solution.py:703
  41.9 0.0 collective-permute-done.1
  41.9 0.0 collective-permute-done
  41.9 0.0 all-to-all-done.1.refs_3_
  41.9 0.0 copy-done.1
  41.9 0.0 copy-done.2
  41.9 46.2 %muscl_final.1 = (f32[4,8192,128]{2,1,0:T(8,128)}, f32[8192,128]{1,0:T(8,128)}) custom-call(f32[4,8192,128]{2,1,0:T(8,128)} %bitcast.29, f32[4,128,128]{2,1,0:T(8,128)S(1)} %bitcast.24, f32[4,128,128]{2,1,0:T(8,128)S(1)} %bitcast.23, f32[8,2,8,128]{3,2,1,0:T(8,128)S(1)} %all-to-all-done.1.refs_3_, ...), custom_call_target="tpu_custom_call", output_to_operand_aliasing={{0}: (6, {})} | custom-call | flops 1277952000 | bytes 27262976 | tf_op jit(solution)/shard_map/muscl_final/pallas_call | solution.py:703
  (2 shorter events, 0.0 us)
Async XLA Ops:
  0.6 21.3 %copy-start = (f32[16,16]{1,0:T(8,128)S(1)}, f32[16,16]{1,0:T(8,128)}, u32[]{:S(2)}) copy-start(f32[16,16]{1,0:T(8,128)} %param.8) | copy-start | bytes 3076
  7.7 15.5 %all-to-all-start = ((f32[32,8,128]{2,1,0:T(8,128)}), f32[32,8,128]{2,1,0:T(8,128)S(1)}, u32[]{:S(2)}, u32[]{:S(2)}) async-start(f32[32,8,128]{2,1,0:T(8,128)} %bitcast.31), calls=%async_computation | async-start | bytes 262144 | tf_op jit(solution)/shard_map/all_to_all | solution.py:752
  16.1 25.8 %collective-permute-start.1 = (f32[4,2,64,128]{3,2,1,0:T(8,128)S(1)}, f32[4,2,64,128]{3,2,1,0:T(8,128)S(1)}, u32[]{:S(2)}, u32[]{:S(2)}) collective-permute-start(f32[4,2,64,128]{3,2,1,0:T(8,128)S(1)} %get-tuple-element.6), channel_id=1, source_target_pairs={{4,0},{8,4},{12,8},{16,12},{20,16},{24,20},{28,24},{5,1},{9,5},{13... | collective-permute-start | bytes 786440 | tf_op jit(solution)/shard_map/ppermute | solution.py:734
  17.4 24.5 %collective-permute-start = (f32[4,2,64,128]{3,2,1,0:T(8,128)S(1)}, f32[4,2,64,128]{3,2,1,0:T(8,128)S(1)}, u32[]{:S(2)}, u32[]{:S(2)}) collective-permute-start(f32[4,2,64,128]{3,2,1,0:T(8,128)S(1)} %get-tuple-element.7), channel_id=1, source_target_pairs={{0,4},{4,8},{8,12},{12,16},{16,20},{20,24},{24,28},{1,5},{5,9},{9,... | collective-permute-start | bytes 786440 | tf_op jit(solution)/shard_map/ppermute | solution.py:733
  23.2 1.6 %copy-start.3 = (bf16[1,1024,1024]{2,1,0:T(8,128)(2,1)S(1)}, bf16[1,1024,1024]{2,1,0:T(8,128)(2,1)}, u32[]{:S(2)}) copy-start(bf16[1,1024,1024]{2,1,0:T(8,128)(2,1)} %green_ref.1) | copy-start | bytes 6291460
  26.3 15.6 %all-to-all-start.1 = ((f32[8,2,8,128]{3,2,1,0:T(8,128)}), f32[8,2,8,128]{3,2,1,0:T(8,128)S(1)}, u32[]{:S(2)}, u32[]{:S(2)}) async-start(f32[8,2,8,128]{3,2,1,0:T(8,128)} %green.1), calls=%async_computation.1 | async-start | bytes 131072 | tf_op jit(solution)/shard_map/all_to_all | solution.py:769
  31.1 10.8 %copy-start.1 = (bf16[256,1024]{1,0:T(8,128)(2,1)S(1)}, bf16[256,1024]{1,0:T(8,128)(2,1)}, u32[]{:S(2)}) copy-start(bf16[256,1024]{1,0:T(8,128)(2,1)} %constant.18.clone.refs_5_) | copy-start | bytes 1572868
  31.1 10.8 %copy-start.2 = (bf16[256,1024]{1,0:T(8,128)(2,1)S(1)}, bf16[256,1024]{1,0:T(8,128)(2,1)}, u32[]{:S(2)}) copy-start(bf16[256,1024]{1,0:T(8,128)(2,1)} %constant.17.clone.refs_4_) | copy-start | bytes 1572868

commit v2 on v1

--- a/solution.py
+++ b/solution.py
@@ -212,9 +212,9 @@
     return table.reshape(2 * LANES, tiles * LANES)
 
 
-def split3(values):
+def split(values, count):
     parts = []
-    for _ in range(3):
+    for _ in range(count):
         part = values.astype(jnp.bfloat16)
         parts.append(part)
         values = values - part.astype(jnp.float32)
@@ -239,7 +239,7 @@
             axis=1,
         )
         table = table_ref[t * LANES : (t + 2) * LANES, :]
-        for part in split3(cells):
+        for part in split(cells, 2):
             term = jnp.dot(part, table, preferred_element_type=jnp.float32)
             total = term if total is None else total + term
     sums_ref[pl.ds(pl.multiple_of(step * rows * SUBS, SUBS), rows * SUBS), :] = total
@@ -293,9 +293,8 @@
 
 
 def face_flux(left, right, normal):
-    inverse = 1.0 / (left[0] * right[0])
-    speed_left = left[normal] * (right[0] * inverse)
-    speed_right = right[normal] * (left[0] * inverse)
+    speed_left = left[normal] / left[0]
+    speed_right = right[normal] / right[0]
     reach = jnp.maximum(jnp.abs(speed_left), jnp.abs(speed_right)) + math.sqrt(sound_sq)
     weight_left = speed_left + reach
     weight_right = speed_right - reach
@@ -304,28 +303,39 @@
     return fluxes
 
 
-def block_step(cell, base_row, constants, scratch, store, pull, fresh):
+def turned_lanes(chunk, ahead):
+    lane = lane_of(chunk.shape) % (LANES // 2)
+    if ahead:
+        return jnp.where(
+            lane >= LANES // 2 - HALF,
+            pltpu.roll(chunk, LANES // 2 - HALF, 1),
+            pltpu.roll(chunk, LANES - HALF, 1),
+        )
+    return jnp.where(
+        lane < HALF, pltpu.roll(chunk, LANES // 2 + HALF, 1), pltpu.roll(chunk, HALF, 1)
+    )
+
+
+def block_step(raw, base_rows, constants, scratch, store, fresh, prepare):
     rows, subs, radial_step, phi_step, step_time = constants
-    d_ref, r_ref, g_ref, w_ref, l_ref, f_ref = scratch
-    tiles = subs // SUBS
-    lane = lane_of((SUBS, LANES))
-    first = lane == 0
-    last = lane == LANES - 1
-
-    def up(here, there):
-        return pltpu.roll(jnp.where(first, there, here), LANES - 1, 1)
-
-    def down(here, there):
-        return pltpu.roll(jnp.where(last, there, here), 1, 1)
-
-    def span(k, shift):
-        return pl.ds(k * SUBS + SUBS + shift, SUBS)
-
-    def radial_face(r, k):
-        part = pl.ds(k * SUBS, SUBS)
+    t_ref, r_ref, g_ref, o_ref, l_ref, f_ref = scratch
+    chunks = LANES // SUBS
+
+    def bring(r):
+        for f in range(4):
+            both = jnp.concatenate([raw(f, 0, r), raw(f, 1, r)], axis=0).T
+            t_ref[r % rows, f, SUBS : SUBS + LANES, :] = both
+            t_ref[r % rows, f, SUBS + LANES :, :] = turned_lanes(both[:SUBS], True)
+            t_ref[r % rows, f, :SUBS, :] = turned_lanes(both[LANES - SUBS :], False)
+
+    def cell(f, r, q, shift=0):
+        return t_ref[r % rows, f, pl.ds(SUBS + q * SUBS + shift, SUBS), :]
+
+    def radial_face(r, q):
+        part = pl.ds(q * SUBS, SUBS)
         left, right = [], []
         for f in range(4):
-            here, above, far = cell(f, r, k), cell(f, r + 1, k), cell(f, r + 2, k)
+            here, above, far = cell(f, r, q), cell(f, r + 1, q), cell(f, r + 2, q)
             slope = limited(above - here, far - above)
             twice = above + above
             left.append(l_ref[f, part, :])
@@ -335,76 +345,75 @@
 
     @pl.when(fresh)
     def _():
-        for k in range(tiles):
-            part = pl.ds(k * SUBS, SUBS)
+        for r in range(-2, 2):
+            bring(r)
+        for q in range(chunks):
+            part = pl.ds(q * SUBS, SUBS)
             for f in range(4):
-                lower, here, above = cell(f, -2, k), cell(f, -1, k), cell(f, 0, k)
+                lower, here, above = cell(f, -2, q), cell(f, -1, q), cell(f, 0, q)
                 l_ref[f, part, :] = (here + here) + limited(here - lower, above - here)
-            for f, value in enumerate(radial_face(-1, k)):
+            for f, value in enumerate(radial_face(-1, q)):
                 f_ref[f, part, :] = value
 
+    prepare()
+    half = lane_of((SUBS, LANES)) < LANES // 2
     for r in range(rows):
         slot = r % 2
-        index = (base_row + r).astype(jnp.float32)
-        centre = inner_radius + (jnp.full((SUBS, LANES), index, jnp.float32) + 0.5) * radial_step
+        bring(r + 2)
+        index = jnp.where(half, base_rows[0] + r, base_rows[1] + r).astype(jnp.float32)
+        centre = inner_radius + (index + 0.5) * radial_step
         over = step_time / centre
         scale = over * (0.25 / radial_step)
         outer = scale * (centre + 0.5 * radial_step)
         inner = scale * (centre - 0.5 * radial_step)
         turn = over * (0.25 / phi_step)
-        for k in range(tiles):
+
+        def edges(q):
+            lefts = []
             for f in range(4):
-                here = cell(f, r, k)
-                if k + 1 < tiles:
-                    there = cell(f, r, k, HALF)
-                else:
-                    there = jnp.concatenate(
-                        [cell(f, r, k)[HALF:], cell(f, r, 0)[:HALF]], axis=0
-                    )
-                delta = up(here, there) - here
-                d_ref[slot, f, span(k, 0), :] = delta
-                if k == tiles - 1:
-                    d_ref[slot, f, HALF:SUBS, :] = delta[HALF:]
-        for k in range(tiles):
-            for f in range(4):
-                here = cell(f, r, k)
-                ahead = d_ref[slot, f, span(k, 0), :]
-                behind = down(ahead, d_ref[slot, f, span(k, -HALF), :])
-                slope = limited(behind, ahead)
+                here = cell(f, r, q)
+                slope = limited(here - cell(f, r, q, -1), cell(f, r, q, 1) - here)
                 twice = here + here
-                w_ref[slot, f, span(k, 0), :] = twice + slope
+                lefts.append(twice + slope)
                 right = twice - slope
-                r_ref[slot, f, span(k, 0), :] = right
-                if k == 0:
-                    r_ref[slot, f, pl.ds(SUBS + subs, HALF), :] = right[:HALF]
-        for k in range(tiles):
-            left = [w_ref[slot, f, span(k, 0), :] for f in range(4)]
-            right = [
-                up(r_ref[slot, f, span(k, 0), :], r_ref[slot, f, span(k, HALF), :])
-                for f in range(4)
-            ]
-            for f, value in enumerate(face_flux(left, right, 2)):
-                g_ref[slot, f, span(k, 0), :] = value
-                if k == tiles - 1:
-                    g_ref[slot, f, HALF:SUBS, :] = value[HALF:]
-        for k in range(tiles):
-            part = pl.ds(k * SUBS, SUBS)
-            radial = radial_face(r, k)
-            values = [cell(f, r, k) for f in range(4)]
+                r_ref[slot, f, pl.ds(q * SUBS, SUBS), :] = right
+                if q == 0:
+                    r_ref[slot, f, pl.ds(LANES, SUBS), :] = turned_lanes(right, True)
+            return lefts
+
+        def finish(q, fluxes):
+            part = pl.ds(q * SUBS, SUBS)
+            radial = radial_face(r, q)
+            values = [cell(f, r, q) for f in range(4)]
             density, push, swing, _ = values
             spin = swing / density
             extra = [None, (swing * spin + sound_sq * density) * over, (push * spin) * -over, None]
             for f, value in enumerate(values):
-                flux = g_ref[slot, f, span(k, 0), :]
-                before = down(flux, g_ref[slot, f, span(k, -HALF), :])
+                before = g_ref[slot, f, pl.ds(SUBS + q * SUBS - 1, SUBS), :]
                 value = value + (inner * f_ref[f, part, :] - outer * radial[f])
-                value = value - turn * (flux - before)
+                value = value - turn * (fluxes[f] - before)
                 if extra[f] is not None:
                     value = value + extra[f]
-                    if pull is not None:
-                        value = value - density * pull(f - 1, r, k)
                 f_ref[f, part, :] = radial[f]
-                store(f, r, k, value)
+                o_ref[slot, f, part, :] = value
+
+        lefts = edges(0)
+        for q in range(chunks):
+            later = edges(q + 1) if q + 1 < chunks else None
+            right = [r_ref[slot, f, pl.ds(q * SUBS + 1, SUBS), :] for f in range(4)]
+            fluxes = face_flux(lefts, right, 2)
+            for f in range(4):
+                g_ref[slot, f, pl.ds(SUBS + q * SUBS, SUBS), :] = fluxes[f]
+                if q == chunks - 1:
+                    g_ref[slot, f, :SUBS, :] = turned_lanes(fluxes[f], False)
+            if q > 0:
+                finish(q, fluxes)
+            lefts = later
+        finish(0, [g_ref[slot, f, SUBS : 2 * SUBS, :] for f in range(4)])
+        for f in range(4):
+            both = o_ref[slot, f].T
+            for h in range(2):
+                store(f, h, r, both[h * subs : (h + 1) * subs])
 
 
 def spectral_rows(modes_ref, left_ref, radial_step, step_time):
@@ -428,7 +437,7 @@
             kinds[1].append((above - below) * (step_time / (2.0 * radial_step)))
             kinds[2].append(here * over)
         for kind, halves in enumerate(kinds):
-            parts = [part.astype(jnp.float32) for part in split3(jnp.concatenate(halves, axis=0))]
+            parts = [part.astype(jnp.float32) for part in split(jnp.concatenate(halves, axis=0), 3)]
             stack = [parts[left] for left, _ in PAIRS]
             stack += [jnp.zeros((LANES - len(PAIRS) * width, LANES), jnp.float32)]
             turned = jnp.concatenate(stack, axis=0).T
@@ -440,17 +449,17 @@
     rows, subs, radii, radial_all, start, count, done = plan
     if final:
         cells, low, high, modes_ref, pot_table, turn_table, old, out, pot_out, *refs = refs
-        left_ref, pull_ref, pot_buf, late_buf, pot_sem, late_sem, *refs = refs
+        left_ref, pull_ref, pot_buf, late_buf, late_pot, pot_sem, late_sem, *refs = refs
     else:
         cells, out, *refs = refs
-    in_buf, out_buf, in_sem, out_sem, *scratch = refs
+    in_buf, out_buf, in_sem, head_sem, out_sem, *scratch = refs
     azimuth = subs // HALF * LANES
     phi_step = 2.0 * math.pi / azimuth
     radial_step = radial_span / radial_all
     step_time = courant * min(radial_step, inner_radius * phi_step)
-    blocks = radii // rows
+    span = radii // 2
+    blocks = span // rows
     size = rows * subs
-    full = (rows + 4) * subs
     position = lax.axis_index("row")
     last_rank = lax.axis_size("row") - 1
     tiles = subs // SUBS
@@ -458,107 +467,176 @@
     def place(n):
         return lax.rem(start + n, blocks)
 
-    def copy_in(source, f, first, length, slot, offset):
+    def line(row):
+        return pl.multiple_of(row * subs, subs)
+
+    def copy_in(source, f, h, row, count_rows, slot, offset, sem):
         return pltpu.make_async_copy(
-            source.at[f, pl.ds(first, length), :],
-            in_buf.at[slot, f, pl.ds(offset, length), :],
-            in_sem.at[slot],
+            source.at[f, pl.ds(line(row), count_rows * subs), :],
+            in_buf.at[slot, f, h, pl.ds(offset * subs, count_rows * subs), :],
+            sem,
         )
 
     def fetch(n, slot):
         b = place(n)
-        base = pl.multiple_of(b * size, size)
-        inside = (b > 0) & (b < blocks - 1)
-
-        @pl.when(inside)
+        first = b * rows
+        lowest = b == 0
+        highest = b == blocks - 1
+        sem = in_sem.at[slot]
+        head_one = head_sem.at[0]
+
+        for f in range(4):
+            copy_in(cells, f, 0, first, rows + 2, slot, 2, sem).start()
+
+        @pl.when(jnp.logical_not(highest))
         def _():
             for f in range(4):
-                copy_in(cells, f, base - 2 * subs, full, slot, 0).start()
+                copy_in(cells, f, 1, span + first, rows + 2, slot, 2, sem).start()
+
+        @pl.when((n == 0) | lowest)
+        def _():
+            for f in range(4):
+                copy_in(cells, f, 1, span + first - 2, 2, slot, 0, head_one).start()
+
+        @pl.when((n == 0) & jnp.logical_not(lowest))
+        def _():
+            for f in range(4):
+                copy_in(cells, f, 0, first - 2, 2, slot, 0, head_one).start()
 
         if not final:
             return
 
-        @pl.when(b == 0)
+        @pl.when(highest)
         def _():
             for f in range(4):
-                copy_in(cells, f, 0, size + 2 * subs, slot, 2 * subs).start()
-
+                copy_in(cells, f, 1, radii - rows, rows, slot, 2, sem).start()
+
+            @pl.when(position == last_rank)
+            def _():
+                for f in range(4):
+                    for i in range(2):
+                        copy_in(cells, f, 1, radii - 1, 1, slot, 2 + rows + i, sem).start()
+
+            @pl.when(position != last_rank)
+            def _():
+                for f in range(4):
+                    copy_in(high, f, 1, 0, 2, slot, 2 + rows, sem).start()
+
+        @pl.when(lowest)
+        def _():
             @pl.when(position == 0)
             def _():
                 for f in range(4):
-                    for h in range(2):
-                        copy_in(cells, f, 0, subs, slot, h * subs).start()
+                    for i in range(2):
+                        copy_in(cells, f, 0, 0, 1, slot, i, head_one).start()
 
             @pl.when(position != 0)
             def _():
                 for f in range(4):
-                    copy_in(low, f, 0, 2 * subs, slot, 0).start()
-
-        @pl.when(b == blocks - 1)
+                    copy_in(low, f, 0, 0, 2, slot, 0, head_one).start()
+
+    def arrived(slot, fresh):
+        for f in range(4):
+            for h in range(2):
+                copy_in(cells, f, h, 0, rows + 2, slot, 2, in_sem.at[slot]).wait()
+
+        @pl.when(fresh)
         def _():
             for f in range(4):
-                copy_in(cells, f, (radii - rows - 2) * subs, size + 2 * subs, slot, 0).start()
-
-            @pl.when(position == last_rank)
-            def _():
-                for f in range(4):
-                    for h in range(2):
-                        copy_in(
-                            cells, f, (radii - 1) * subs, subs, slot, size + (2 + h) * subs
-                        ).start()
-
-            @pl.when(position != last_rank)
-            def _():
-                for f in range(4):
-                    copy_in(high, f, 0, 2 * subs, slot, size + 2 * subs).start()
-
-    def arrived(slot):
-        for f in range(4):
-            copy_in(cells, f, 0, full, slot, 0).wait()
-
-    def give(n, slot):
-        base = pl.multiple_of(place(n) * size, size)
-        copies = [
-            pltpu.make_async_copy(
-                out_buf.at[slot, f, pl.ds(0, size), :],
-                out.at[f, pl.ds(base, size), :],
-                out_sem.at[slot],
-            )
-            for f in range(4)
-        ]
-        if final:
+                for h in range(2):
+                    copy_in(cells, f, h, 0, 2, slot, 0, head_sem.at[0]).wait()
+
+    def result(b, slot, fields, sem):
+        copies = []
+        for h in range(2):
+            part = pl.ds(line(h * span + b * rows), size)
+            for f in fields:
+                copies.append(
+                    pltpu.make_async_copy(
+                        out_buf.at[slot, f, h, pl.ds(0, size), :], out.at[f, part, :], sem.at[slot]
+                    )
+                )
+            if final:
+                copies.append(
+                    pltpu.make_async_copy(pot_buf.at[slot, h], pot_out.at[part, :], sem.at[slot])
+                )
+        return copies
+
+    def late_in(n):
+        copies = []
+        for h in range(2):
+            part = pl.ds((h * span + (1 + n) * rows) * subs, size)
+            for i, (source, f) in enumerate(((cells, 0), (out, 1), (out, 2))):
+                copies.append(
+                    pltpu.make_async_copy(
+                        source.at[f, part, :], late_buf.at[n, i, h], late_sem.at[n]
+                    )
+                )
+        return copies
+
+    def late_out(n):
+        copies = []
+        for h in range(2):
+            part = pl.ds((h * span + (1 + n) * rows) * subs, size)
+            for f in (1, 2):
+                copies.append(
+                    pltpu.make_async_copy(late_buf.at[n, f, h], out.at[f, part, :], pot_sem.at[n])
+                )
             copies.append(
-                pltpu.make_async_copy(
-                    pot_buf.at[slot], pot_out.at[pl.ds(base, size), :], out_sem.at[slot]
-                )
+                pltpu.make_async_copy(late_pot.at[n, h], pot_out.at[part, :], pot_sem.at[n])
             )
         return copies
 
     fetch(0, 0)
     if final:
+        for n in range(done):
+            for copy in late_in(n):
+                copy.start()
         spectral_rows(modes_ref, left_ref, radial_step, step_time)
 
-    def spectral(b, pot_slot):
-        span = pl.ds(pl.multiple_of(b * rows * SUBS, SUBS), rows * SUBS)
+    def spectral(b, pot_here):
+        lines = [
+            pl.ds((h * span + b * rows) * SUBS if isinstance(b, int) else pl.multiple_of((h * span + b * rows) * SUBS, SUBS), rows * SUBS)
+            for h in range(2)
+        ]
 
         def product(kinds, table):
             left = [
-                jnp.concatenate([left_ref[kind, p, span, :] for p in range(2)], axis=1)
+                jnp.concatenate([left_ref[kind, p, where, :] for p in range(2)], axis=1)
                 for kind in kinds
+                for where in lines
             ]
             left = jnp.concatenate(left, axis=0).astype(jnp.bfloat16)
             return jnp.dot(left, table[...], preferred_element_type=jnp.float32)
 
         both = product((0, 1), pot_table)
         turn = product((2,), turn_table)
-        for r in range(rows):
-            for t in range(tiles):
-                part = pl.ds(r * subs + t * SUBS, SUBS)
-                column = slice(t * LANES, (t + 1) * LANES)
-                line = slice(r * SUBS, (r + 1) * SUBS)
-                pot_buf[pot_slot, part, :] = both[line, column]
-                pull_ref[0, part, :] = both[rows * SUBS + r * SUBS : rows * SUBS + (r + 1) * SUBS, column]
-                pull_ref[1, part, :] = turn[line, column]
+        for h in range(2):
+            for r in range(rows):
+                low_line = (h * rows + r) * SUBS
+                pull_line = ((2 + h) * rows + r) * SUBS
+                for t in range(tiles):
+                    part = pl.ds(r * subs + t * SUBS, SUBS)
+                    column = slice(t * LANES, (t + 1) * LANES)
+                    pot_here[h, part, :] = both[low_line : low_line + SUBS, column]
+                    pull_ref[0, h, part, :] = both[pull_line : pull_line + SUBS, column]
+                    pull_ref[1, h, part, :] = turn[low_line : low_line + SUBS, column]
+
+    if final:
+        for n in range(done):
+            spectral(1 + n, late_pot.at[n])
+            for copy in late_in(n):
+                copy.wait()
+            for h in range(2):
+                for t in range(rows * tiles):
+                    part = pl.ds(t * SUBS, SUBS)
+                    density = late_buf[n, 0, h, part, :]
+                    for f in (1, 2):
+                        late_buf[n, f, h, part, :] = (
+                            late_buf[n, f, h, part, :] - density * pull_ref[f - 1, h, part, :]
+                        )
+            for copy in late_out(n):
+                copy.start()
 
     def body(n, carry):
         slot = lax.rem(n, 2)
@@ -569,100 +647,41 @@
 
         @pl.when(n >= 2)
         def _():
-            for copy in give(n - 2, slot):
+            for copy in result(place(n - 2), slot, range(4), out_sem):
                 copy.wait()
 
         b = place(n)
-        pull = None
-        if final:
-            spectral(b, slot)
-
-            def pull(kind, r, k):
-                return pull_ref[kind, pl.ds(r * subs + k * SUBS, SUBS), :]
-
-        arrived(slot)
-
-        def cell(f, r, k, shift=0):
-            return in_buf[slot, f, pl.ds((r + 2) * subs + k * SUBS + shift, SUBS), :]
-
-        def store(f, r, k, value):
-            out_buf[slot, f, pl.ds(r * subs + k * SUBS, SUBS), :] = value
+        fresh = (n == 0) | (b == 0)
+        arrived(slot, fresh)
+
+        def prepare():
+            if final:
+                spectral(b, pot_buf.at[slot])
+
+        def raw(f, h, r):
+            return in_buf[slot, f, h, pl.ds((r + 2) * subs, subs), :]
+
+        def store(f, h, r, value):
+            part = pl.ds(r * subs, subs)
+            if final and f in (1, 2):
+                value = value - raw(0, h, r) * pull_ref[f - 1, h, part, :]
+            out_buf[slot, f, h, part, :] = value
 
         constants = (rows, subs, radial_step, phi_step, step_time)
-        block_step(
-            cell, position * radii + b * rows, constants, scratch, store, pull, (n == 0) | (b == 0)
-        )
-        for copy in give(n, slot):
+        base = position * radii + b * rows
+        block_step(raw, (base, base + span), constants, scratch, store, fresh, prepare)
+        for copy in result(b, slot, range(4), out_sem):
             copy.start()
         return carry
 
     lax.fori_loop(0, count, body, 0)
     for n in range(max(count - 2, 0), count):
-        for copy in give(n, n % 2):
+        for copy in result(place(n), n % 2, range(4), out_sem):
             copy.wait()
-    if not final:
-        return
-
-    def late_in(n, slot):
-        base = pl.multiple_of((1 + n) * size, size)
-        return [
-            pltpu.make_async_copy(
-                source.at[f, pl.ds(base, size), :], late_buf.at[slot, i], late_sem.at[slot]
-            )
-            for i, (source, f) in enumerate(((cells, 0), (out, 1), (out, 2)))
-        ]
-
-    def late_out(n, slot):
-        base = pl.multiple_of((1 + n) * size, size)
-        copies = [
-            pltpu.make_async_copy(
-                out_buf.at[slot, f, pl.ds(0, size), :],
-                out.at[f, pl.ds(base, size), :],
-                pot_sem.at[slot],
-            )
-            for f in (1, 2)
-        ]
-        copies.append(
-            pltpu.make_async_copy(
-                pot_buf.at[slot], pot_out.at[pl.ds(base, size), :], pot_sem.at[slot]
-            )
-        )
-        return copies
-
-    for copy in late_in(0, 0):
-        copy.start()
-
-    def late(n, carry):
-        slot = lax.rem(n, 2)
-
-        @pl.when(n + 1 < done)
-        def _():
-            for copy in late_in(n + 1, 1 - slot):
-                copy.start()
-
-        @pl.when(n >= 2)
-        def _():
-            for copy in late_out(n - 2, slot):
+    if final:
+        for n in range(done):
+            for copy in late_out(n):
                 copy.wait()
-
-        spectral(1 + n, slot)
-        for copy in late_in(n, slot):
-            copy.wait()
-        for t in range(rows * tiles):
-            part = pl.ds(t * SUBS, SUBS)
-            density = late_buf[slot, 0, part, :]
-            for f in (1, 2):
-                out_buf[slot, f, part, :] = (
-                    late_buf[slot, f, part, :] - density * pull_ref[f - 1, part, :]
-                )
-        for copy in late_out(n, slot):
-            copy.start()
-        return carry
-
-    lax.fori_loop(0, done, late, 0)
-    for n in range(max(done - 2, 0), done):
-        for copy in late_out(n, n % 2):
-            copy.wait()
 
 
 def vmem_limit(mebibytes):
@@ -670,20 +689,24 @@
 
 
 def muscl(operands, plan, final, shape):
-    rows, subs, radii, _, _, count, _ = plan
+    rows, subs, radii, _, _, count, done = plan
     fields = shape[0]
     size = rows * subs
-    pad = subs + 3 * SUBS
     anywhere = pl.BlockSpec(memory_space=pl.ANY)
     whole = pl.BlockSpec(memory_space=pltpu.VMEM)
     carried = [
-        pltpu.VMEM((2, fields, (rows + 4) * subs + SUBS, LANES), jnp.float32),
-        pltpu.VMEM((2, fields, size + SUBS, LANES), jnp.float32),
+        pltpu.VMEM((2, fields, 2, (rows + 4) * subs, LANES), jnp.float32),
+        pltpu.VMEM((2, fields, 2, size, LANES), jnp.float32),
         pltpu.SemaphoreType.DMA((2,)),
+        pltpu.SemaphoreType.DMA((1,)),
         pltpu.SemaphoreType.DMA((2,)),
+        pltpu.VMEM((rows, fields, LANES + 2 * SUBS, LANES), jnp.float32),
+        pltpu.VMEM((2, fields, LANES + SUBS, LANES), jnp.float32),
+        pltpu.VMEM((2, fields, LANES + SUBS, LANES), jnp.float32),
+        pltpu.VMEM((2, fields, LANES, LANES), jnp.float32),
+        pltpu.VMEM((fields, LANES, LANES), jnp.float32),
+        pltpu.VMEM((fields, LANES, LANES), jnp.float32),
     ]
-    carried += [pltpu.VMEM((2, fields, pad, LANES), jnp.float32) for _ in range(4)]
-    carried += [pltpu.VMEM((fields, subs + SUBS, LANES), jnp.float32) for _ in range(2)]
     out_shape = [jax.ShapeDtypeStruct(shape, jnp.float32)]
     if final:
         in_specs = [anywhere] * 3 + [whole] * 3 + [anywhere]
@@ -691,11 +714,12 @@
         aliases = {6: 0}
         carried = [
             pltpu.VMEM((3, 2, radii * SUBS, LANES), jnp.float32),
-            pltpu.VMEM((2, size, LANES), jnp.float32),
-            pltpu.VMEM((2, size, LANES), jnp.float32),
-            pltpu.VMEM((2, 3, size, LANES), jnp.float32),
-            pltpu.SemaphoreType.DMA((2,)),
-            pltpu.SemaphoreType.DMA((2,)),
+            pltpu.VMEM((2, 2, size, LANES), jnp.float32),
+            pltpu.VMEM((2, 2, size, LANES), jnp.float32),
+            pltpu.VMEM((done, 3, 2, size, LANES), jnp.float32),
+            pltpu.VMEM((done, 2, size, LANES), jnp.float32),
+            pltpu.SemaphoreType.DMA((done,)),
+            pltpu.SemaphoreType.DMA((done,)),
         ] + carried
     else:
         in_specs = [anywhere]
@@ -710,8 +734,8 @@
         scratch_shapes=carried,
         compiler_params=vmem_limit(50),
         cost_estimate=pl.CostEstimate(
-            flops=count * rows * subs * LANES * 1500,
-            bytes_accessed=count * size * LANES * 32,
+            flops=count * rows * subs * LANES * 3000,
+            bytes_accessed=count * size * LANES * 64,
             transcendentals=0,
         ),
     )(*operands)
@@ -733,7 +757,7 @@
     low = lax.ppermute(cells[:, radii - 2 :], "row", up_ring)
     high = lax.ppermute(cells[:, :2], "row", [(j, i) for i, j in up_ring])
 
-    rows = 16
+    rows = 32
     spectrum = pl.pallas_call(
         lambda *refs: spectrum_kernel(stacks, *refs),
         name="spectrum",
@@ -768,8 +792,8 @@
     )(gathered.reshape(ranks, stacks * SUBS, LANES), weights, green)
     pot_spec = lax.all_to_all(pot_modes, "row", 0, 0, tiled=True)
 
-    rows, early = 8, 3
-    blocks = radii // rows
+    rows, early = 4, 2
+    blocks = radii // 2 // rows
     flat = cells.reshape(fields, radii * subs, LANES)
     flat_low = low.reshape(fields, 2 * subs, LANES)
     flat_high = high.reshape(fields, 2 * subs, LANES)

time: 88.6 us -> 71.6 us (0.81)
  Pallas kernels: 65.5 us -> 48.6 us
    pallas_call x2, Pallas kernels: 56.9 us -> 42.3 us  [muscl(): pl.pallas_call(lambda *refs: muscl_kernel(plan, final, *refs), name='musc...]
    pallas_call x1, Pallas kernels: 7.06 us -> 4.75 us  [fast_body(): pl.pallas_call(lambda *refs: spectrum_kernel(stacks, *refs), name='spectr...]
  transfers between devices with their start and end apart: 4 -> 4, of which waited for: 1 -> 1; matrix products, arithmetic and copies ran while one was open for 2% -> 2% of each run, Pallas kernels for 14% -> 12%
where the time goes in v2:
time: 71.6 us; the launch traced here: 71.2 us
  Pallas kernels  48.6 us (68%)
  starting transfers between devices  18 us (25%)
  local copies, waits for them, and re-layouts  2.88 us (4%)
  waiting for transfers between devices  0.95 us (1%)
  between operations  0.76 us (1%)
    pallas_call x2, Pallas kernels, muscl(): pl.pallas_call(lambda *refs: muscl_kernel(plan, final, *refs), name='musc...  42.3 us
    all_to_all x1, starting transfers between devices, fast_body(): lax.all_to_all(spectrum.reshape(ranks * stacks, SUBS, LANES), ('row', 'gz...  7.32 us
    all_to_all x1, starting transfers between devices, fast_body(): pot_spec = lax.all_to_all(pot_modes, 'row', 0, 0, tiled=True)  4.81 us
    pallas_call x1, Pallas kernels, fast_body(): pl.pallas_call(lambda *refs: spectrum_kernel(stacks, *refs), name='spectr...  4.75 us
    ppermute x1, starting transfers between devices, fast_body(): low = lax.ppermute(cells[:, radii - 2:], 'row', up_ring)  4.56 us
    unnamed x8, local copies, waits for them, and re-layouts  1.61 us
    pallas_call x1, Pallas kernels, fast_body(): pl.pallas_call(green_kernel, name='green', in_specs=[pl.BlockSpec(memory_...  1.49 us
  transfers between devices with their start and end apart: 4, of which 1 were waited for; matrix products, arithmetic and copies ran while one was open for 2% of the time, Pallas kernels for 12%

profile of v2, /device:TPU:0, one launch (start us, length us, event | category | flops | bytes accessed | tf_op | source)
XLA Modules:
  0.0 71.2 jit_solution(10815077874561261854)
XLA Ops:
  0.6 0.0 copy-start
  0.6 4.7 %spectrum.1 = f32[8,4,8,128]{3,2,1,0:T(8,128)} custom-call(f32[4,128,64,128]{3,2,1,0:T(8,128)} %bitcast.26, bf16[1024,128]{1,0:T(8,128)(2,1)} %constant.16.clone.refs_1_), custom_call_target="tpu_custom_call" | custom-call | flops 8589934592 | bytes 4194304 | tf_op jit(solution)/shard_map/spectrum/pallas_call | solution.py:761
  5.4 7.3 %all-to-all-start = ((f32[32,8,128]{2,1,0:T(8,128)}), f32[32,8,128]{2,1,0:T(8,128)S(1)}, u32[]{:S(2)}, u32[]{:S(2)}) async-start(f32[32,8,128]{2,1,0:T(8,128)} %bitcast.31), calls=%async_computation | async-start | bytes 262144 | tf_op jit(solution)/shard_map/all_to_all | solution.py:776
  12.7 1.1 %fusion = (f32[4,2,64,128]{3,2,1,0:T(8,128)S(1)}, f32[4,2,64,128]{3,2,1,0:T(8,128)S(1)}) fusion(f32[4,128,64,128]{3,2,1,0:T(8,128)} %bitcast.27), kind=kLoop, calls=%fused_computation.3 | loop fusion | bytes 1048576 | tf_op jit(solution)/shard_map/slice | solution.py:758
  13.8 1.3 %collective-permute-start.1 = (f32[4,2,64,128]{3,2,1,0:T(8,128)S(1)}, f32[4,2,64,128]{3,2,1,0:T(8,128)S(1)}, u32[]{:S(2)}, u32[]{:S(2)}) collective-permute-start(f32[4,2,64,128]{3,2,1,0:T(8,128)S(1)} %get-tuple-element.6), channel_id=1, source_target_pairs={{4,0},{8,4},{12,8},{16,12},{20,16},{24,20},{28,24},{5,1},{9,5},{13... | collective-permute-start | bytes 786440 | tf_op jit(solution)/shard_map/ppermute | solution.py:758
  15.1 4.6 %collective-permute-start = (f32[4,2,64,128]{3,2,1,0:T(8,128)S(1)}, f32[4,2,64,128]{3,2,1,0:T(8,128)S(1)}, u32[]{:S(2)}, u32[]{:S(2)}) collective-permute-start(f32[4,2,64,128]{3,2,1,0:T(8,128)S(1)} %get-tuple-element.7), channel_id=1, source_target_pairs={{0,4},{4,8},{8,12},{12,16},{16,20},{20,24},{24,28},{1,5},{5,9},{9,... | collective-permute-start | bytes 786440 | tf_op jit(solution)/shard_map/ppermute | solution.py:757
  19.7 0.0 copy-done
  19.7 0.1 reshape.46
  19.8 0.1 multiply_bitcast_fusion
  19.9 0.1 reshape.47.weights_ref
  20.0 0.9 %all-to-all-done = f32[32,8,128]{2,1,0:T(8,128)S(1)} async-done(((f32[32,8,128]{2,1,0:T(8,128)}), f32[32,8,128]{2,1,0:T(8,128)S(1)}, u32[]{:S(2)}, u32[]{:S(2)}) %all-to-all-start) | async-done | bytes 131104 | tf_op jit(solution)/shard_map/all_to_all | solution.py:776
  20.9 0.0 copy-start.3
  20.9 1.6 %copy-done.3 = bf16[1,1024,1024]{2,1,0:T(8,128)(2,1)S(1)} copy-done((bf16[1,1024,1024]{2,1,0:T(8,128)(2,1)S(1)}, bf16[1,1024,1024]{2,1,0:T(8,128)(2,1)}, u32[]{:S(2)}) %copy-start.3) | copy-done | bytes 2097176
  22.5 1.5 %green.1 = f32[8,2,8,128]{3,2,1,0:T(8,128)} custom-call(f32[8,32,128]{2,1,0:T(8,128)S(1)} %bitcast.25, f32[8,32]{1,0:T(8,128)S(1)} %reshape.47.weights_ref, bf16[1,1024,1024]{2,1,0:T(8,128)(2,1)S(1)} %copy-done.3), custom_call_target="tpu_custom_call" | custom-call | flops 1073741824 | bytes 2097152 | tf_op jit(solution)/shard_map/green/pallas_call | solution.py:784
  24.0 4.8 %all-to-all-start.1 = ((f32[8,2,8,128]{3,2,1,0:T(8,128)}), f32[8,2,8,128]{3,2,1,0:T(8,128)S(1)}, u32[]{:S(2)}, u32[]{:S(2)}) async-start(f32[8,2,8,128]{3,2,1,0:T(8,128)} %green.1), calls=%async_computation.1 | async-start | bytes 131072 | tf_op jit(solution)/shard_map/all_to_all | solution.py:793
  28.8 0.0 copy-start.1
  28.8 0.0 copy-start.2
  28.8 7.2 %muscl_early.1.refs_6_ = f32[4,8192,128]{2,1,0:T(8,128)} custom-call(f32[4,8192,128]{2,1,0:T(8,128)} %bitcast.28), custom_call_target="tpu_custom_call" | custom-call | flops 196608000 | bytes 4194304 | tf_op jit(solution)/shard_map/muscl_early/pallas_call | solution.py:727
  36.0 0.0 collective-permute-done.1
  36.0 0.0 collective-permute-done
  36.1 0.0 all-to-all-done.1.refs_3_
  36.1 0.0 copy-done.1
  36.1 0.0 copy-done.2
  36.1 35.1 %muscl_final.1 = (f32[4,8192,128]{2,1,0:T(8,128)}, f32[8192,128]{1,0:T(8,128)}) custom-call(f32[4,8192,128]{2,1,0:T(8,128)} %bitcast.29, f32[4,128,128]{2,1,0:T(8,128)S(1)} %bitcast.24, f32[4,128,128]{2,1,0:T(8,128)S(1)} %bitcast.23, f32[8,2,8,128]{3,2,1,0:T(8,128)S(1)} %all-to-all-done.1.refs_3_, ...), custom_call_target="tpu_custom_call", output_to_operand_aliasing={{0}: (6, {})} | custom-call | flops 1376256000 | bytes 29360128 | tf_op jit(solution)/shard_map/muscl_final/pallas_call | solution.py:727
  (2 shorter events, 0.0 us)
Async XLA Ops:
  0.6 19.1 %copy-start = (f32[16,16]{1,0:T(8,128)S(1)}, f32[16,16]{1,0:T(8,128)}, u32[]{:S(2)}) copy-start(f32[16,16]{1,0:T(8,128)} %param.8) | copy-start | bytes 3076
  5.4 15.5 %all-to-all-start = ((f32[32,8,128]{2,1,0:T(8,128)}), f32[32,8,128]{2,1,0:T(8,128)S(1)}, u32[]{:S(2)}, u32[]{:S(2)}) async-start(f32[32,8,128]{2,1,0:T(8,128)} %bitcast.31), calls=%async_computation | async-start | bytes 262144 | tf_op jit(solution)/shard_map/all_to_all | solution.py:776
  13.8 22.2 %collective-permute-start.1 = (f32[4,2,64,128]{3,2,1,0:T(8,128)S(1)}, f32[4,2,64,128]{3,2,1,0:T(8,128)S(1)}, u32[]{:S(2)}, u32[]{:S(2)}) collective-permute-start(f32[4,2,64,128]{3,2,1,0:T(8,128)S(1)} %get-tuple-element.6), channel_id=1, source_target_pairs={{4,0},{8,4},{12,8},{16,12},{20,16},{24,20},{28,24},{5,1},{9,5},{13... | collective-permute-start | bytes 786440 | tf_op jit(solution)/shard_map/ppermute | solution.py:758
  15.1 20.9 %collective-permute-start = (f32[4,2,64,128]{3,2,1,0:T(8,128)S(1)}, f32[4,2,64,128]{3,2,1,0:T(8,128)S(1)}, u32[]{:S(2)}, u32[]{:S(2)}) collective-permute-start(f32[4,2,64,128]{3,2,1,0:T(8,128)S(1)} %get-tuple-element.7), channel_id=1, source_target_pairs={{0,4},{4,8},{8,12},{12,16},{16,20},{20,24},{24,28},{1,5},{5,9},{9,... | collective-permute-start | bytes 786440 | tf_op jit(solution)/shard_map/ppermute | solution.py:757
  20.9 1.6 %copy-start.3 = (bf16[1,1024,1024]{2,1,0:T(8,128)(2,1)S(1)}, bf16[1,1024,1024]{2,1,0:T(8,128)(2,1)}, u32[]{:S(2)}) copy-start(bf16[1,1024,1024]{2,1,0:T(8,128)(2,1)} %green_ref.1) | copy-start | bytes 6291460
  24.0 12.1 %all-to-all-start.1 = ((f32[8,2,8,128]{3,2,1,0:T(8,128)}), f32[8,2,8,128]{3,2,1,0:T(8,128)S(1)}, u32[]{:S(2)}, u32[]{:S(2)}) async-start(f32[8,2,8,128]{3,2,1,0:T(8,128)} %green.1), calls=%async_computation.1 | async-start | bytes 131072 | tf_op jit(solution)/shard_map/all_to_all | solution.py:793
  28.8 7.3 %copy-start.1 = (bf16[256,1024]{1,0:T(8,128)(2,1)S(1)}, bf16[256,1024]{1,0:T(8,128)(2,1)}, u32[]{:S(2)}) copy-start(bf16[256,1024]{1,0:T(8,128)(2,1)} %constant.18.clone.refs_5_) | copy-start | bytes 1572868
  28.8 7.3 %copy-start.2 = (bf16[256,1024]{1,0:T(8,128)(2,1)S(1)}, bf16[256,1024]{1,0:T(8,128)(2,1)}, u32[]{:S(2)}) copy-start(bf16[256,1024]{1,0:T(8,128)(2,1)} %constant.17.clone.refs_4_) | copy-start | bytes 1572868

commit v3 on v2

--- a/solution.py
+++ b/solution.py
@@ -318,7 +318,7 @@
 
 def block_step(raw, base_rows, constants, scratch, store, fresh, prepare):
     rows, subs, radial_step, phi_step, step_time = constants
-    t_ref, r_ref, g_ref, o_ref, l_ref, f_ref = scratch
+    t_ref, r_ref, g_ref, o_ref, l_ref, f_ref, s_ref = scratch
     chunks = LANES // SUBS
 
     def bring(r):
@@ -335,16 +335,22 @@
         part = pl.ds(q * SUBS, SUBS)
         left, right = [], []
         for f in range(4):
-            here, above, far = cell(f, r, q), cell(f, r + 1, q), cell(f, r + 2, q)
-            slope = limited(above - here, far - above)
+            above = cell(f, r + 1, q)
+            ahead = cell(f, r + 2, q) - above
+            slope = limited(s_ref[f, part, :], ahead)
+            s_ref[f, part, :] = ahead
             twice = above + above
             left.append(l_ref[f, part, :])
             right.append(twice - slope)
             l_ref[f, part, :] = twice + slope
         return face_flux(left, right, 1)
 
+    half = lane_of((SUBS, LANES)) < LANES // 2
+
     @pl.when(fresh)
     def _():
+        lowest = jnp.where(half, base_rows[0], base_rows[1]).astype(jnp.float32)
+        first_weight = (inner_radius + lowest * radial_step) * (phi_step / radial_step)
         for r in range(-2, 2):
             bring(r)
         for q in range(chunks):
@@ -352,21 +358,19 @@
             for f in range(4):
                 lower, here, above = cell(f, -2, q), cell(f, -1, q), cell(f, 0, q)
                 l_ref[f, part, :] = (here + here) + limited(here - lower, above - here)
+                s_ref[f, part, :] = above - here
             for f, value in enumerate(radial_face(-1, q)):
-                f_ref[f, part, :] = value
+                f_ref[f, part, :] = value * first_weight
 
     prepare()
-    half = lane_of((SUBS, LANES)) < LANES // 2
     for r in range(rows):
         slot = r % 2
         bring(r + 2)
         index = jnp.where(half, base_rows[0] + r, base_rows[1] + r).astype(jnp.float32)
         centre = inner_radius + (index + 0.5) * radial_step
         over = step_time / centre
-        scale = over * (0.25 / radial_step)
-        outer = scale * (centre + 0.5 * radial_step)
-        inner = scale * (centre - 0.5 * radial_step)
         turn = over * (0.25 / phi_step)
+        weight = (centre + 0.5 * radial_step) * (phi_step / radial_step)
 
         def edges(q):
             lefts = []
@@ -387,14 +391,16 @@
             values = [cell(f, r, q) for f in range(4)]
             density, push, swing, _ = values
             spin = swing / density
-            extra = [None, (swing * spin + sound_sq * density) * over, (push * spin) * -over, None]
+            spin = spin * (4.0 * phi_step)
+            extra = [None, swing * spin + density * (4.0 * phi_step * sound_sq), push * -spin, None]
             for f, value in enumerate(values):
                 before = g_ref[slot, f, pl.ds(SUBS + q * SUBS - 1, SUBS), :]
-                value = value + (inner * f_ref[f, part, :] - outer * radial[f])
-                value = value - turn * (fluxes[f] - before)
+                face = weight * radial[f]
+                change = (f_ref[f, part, :] - face) + (before - fluxes[f])
                 if extra[f] is not None:
-                    value = value + extra[f]
-                f_ref[f, part, :] = radial[f]
+                    change = change + extra[f]
+                value = value + turn * change
+                f_ref[f, part, :] = face
                 o_ref[slot, f, part, :] = value
 
         lefts = edges(0)
@@ -704,6 +710,7 @@
         pltpu.VMEM((2, fields, LANES + SUBS, LANES), jnp.float32),
         pltpu.VMEM((2, fields, LANES + SUBS, LANES), jnp.float32),
         pltpu.VMEM((2, fields, LANES, LANES), jnp.float32),
+        pltpu.VMEM((fields, LANES, LANES), jnp.float32),
         pltpu.VMEM((fields, LANES, LANES), jnp.float32),
         pltpu.VMEM((fields, LANES, LANES), jnp.float32),
     ]

time: 71.6 us -> 70.8 us (0.989)
  Pallas kernels: 48.6 us -> 47.7 us
    pallas_call x2, Pallas kernels: 42.3 us -> 41.5 us  [muscl(): pl.pallas_call(lambda *refs: muscl_kernel(plan, final, *refs), name='musc...]
where the time goes in v3:
time: 70.8 us; the launch traced here: 70.4 us
  Pallas kernels  47.7 us (67%)
  starting transfers between devices  18 us (25%)
  local copies, waits for them, and re-layouts  2.88 us (4%)
  waiting for transfers between devices  0.95 us (1%)
  between operations  0.76 us (1%)
    pallas_call x2, Pallas kernels, muscl(): pl.pallas_call(lambda *refs: muscl_kernel(plan, final, *refs), name='musc...  41.5 us
    all_to_all x1, starting transfers between devices, fast_body(): lax.all_to_all(spectrum.reshape(ranks * stacks, SUBS, LANES), ('row', 'gz...  7.32 us
    all_to_all x1, starting transfers between devices, fast_body(): pot_spec = lax.all_to_all(pot_modes, 'row', 0, 0, tiled=True)  4.81 us
    pallas_call x1, Pallas kernels, fast_body(): pl.pallas_call(lambda *refs: spectrum_kernel(stacks, *refs), name='spectr...  4.75 us
    ppermute x1, starting transfers between devices, fast_body(): low = lax.ppermute(cells[:, radii - 2:], 'row', up_ring)  4.56 us
    unnamed x8, local copies, waits for them, and re-layouts  1.61 us
    pallas_call x1, Pallas kernels, fast_body(): pl.pallas_call(green_kernel, name='green', in_specs=[pl.BlockSpec(memory_...  1.49 us
  transfers between devices with their start and end apart: 4, of which 1 were waited for; matrix products, arithmetic and copies ran while one was open for 2% of the time, Pallas kernels for 12%

profile of v3, /device:TPU:0, one launch (start us, length us, event | category | flops | bytes accessed | tf_op | source)
XLA Modules:
  0.0 70.4 jit_solution(16358539569985263918)
XLA Ops:
  0.6 0.0 copy-start
  0.6 4.7 %spectrum.1 = f32[8,4,8,128]{3,2,1,0:T(8,128)} custom-call(f32[4,128,64,128]{3,2,1,0:T(8,128)} %bitcast.26, bf16[1024,128]{1,0:T(8,128)(2,1)} %constant.16.clone.refs_1_), custom_call_target="tpu_custom_call" | custom-call | flops 8589934592 | bytes 4194304 | tf_op jit(solution)/shard_map/spectrum/pallas_call | solution.py:768
  5.4 7.3 %all-to-all-start = ((f32[32,8,128]{2,1,0:T(8,128)}), f32[32,8,128]{2,1,0:T(8,128)S(1)}, u32[]{:S(2)}, u32[]{:S(2)}) async-start(f32[32,8,128]{2,1,0:T(8,128)} %bitcast.31), calls=%async_computation | async-start | bytes 262144 | tf_op jit(solution)/shard_map/all_to_all | solution.py:783
  12.7 1.1 %fusion = (f32[4,2,64,128]{3,2,1,0:T(8,128)S(1)}, f32[4,2,64,128]{3,2,1,0:T(8,128)S(1)}) fusion(f32[4,128,64,128]{3,2,1,0:T(8,128)} %bitcast.27), kind=kLoop, calls=%fused_computation.3 | loop fusion | bytes 1048576 | tf_op jit(solution)/shard_map/slice | solution.py:765
  13.8 1.3 %collective-permute-start.1 = (f32[4,2,64,128]{3,2,1,0:T(8,128)S(1)}, f32[4,2,64,128]{3,2,1,0:T(8,128)S(1)}, u32[]{:S(2)}, u32[]{:S(2)}) collective-permute-start(f32[4,2,64,128]{3,2,1,0:T(8,128)S(1)} %get-tuple-element.6), channel_id=1, source_target_pairs={{4,0},{8,4},{12,8},{16,12},{20,16},{24,20},{28,24},{5,1},{9,5},{13... | collective-permute-start | bytes 786440 | tf_op jit(solution)/shard_map/ppermute | solution.py:765
  15.1 4.6 %collective-permute-start = (f32[4,2,64,128]{3,2,1,0:T(8,128)S(1)}, f32[4,2,64,128]{3,2,1,0:T(8,128)S(1)}, u32[]{:S(2)}, u32[]{:S(2)}) collective-permute-start(f32[4,2,64,128]{3,2,1,0:T(8,128)S(1)} %get-tuple-element.7), channel_id=1, source_target_pairs={{0,4},{4,8},{8,12},{12,16},{16,20},{20,24},{24,28},{1,5},{5,9},{9,... | collective-permute-start | bytes 786440 | tf_op jit(solution)/shard_map/ppermute | solution.py:764
  19.7 0.0 copy-done
  19.7 0.1 reshape.46
  19.8 0.1 multiply_bitcast_fusion
  19.9 0.1 reshape.47.weights_ref
  20.0 0.9 %all-to-all-done = f32[32,8,128]{2,1,0:T(8,128)S(1)} async-done(((f32[32,8,128]{2,1,0:T(8,128)}), f32[32,8,128]{2,1,0:T(8,128)S(1)}, u32[]{:S(2)}, u32[]{:S(2)}) %all-to-all-start) | async-done | bytes 131104 | tf_op jit(solution)/shard_map/all_to_all | solution.py:783
  20.9 0.0 copy-start.3
  20.9 1.6 %copy-done.3 = bf16[1,1024,1024]{2,1,0:T(8,128)(2,1)S(1)} copy-done((bf16[1,1024,1024]{2,1,0:T(8,128)(2,1)S(1)}, bf16[1,1024,1024]{2,1,0:T(8,128)(2,1)}, u32[]{:S(2)}) %copy-start.3) | copy-done | bytes 2097176
  22.5 1.5 %green.1 = f32[8,2,8,128]{3,2,1,0:T(8,128)} custom-call(f32[8,32,128]{2,1,0:T(8,128)S(1)} %bitcast.25, f32[8,32]{1,0:T(8,128)S(1)} %reshape.47.weights_ref, bf16[1,1024,1024]{2,1,0:T(8,128)(2,1)S(1)} %copy-done.3), custom_call_target="tpu_custom_call" | custom-call | flops 1073741824 | bytes 2097152 | tf_op jit(solution)/shard_map/green/pallas_call | solution.py:791
  24.0 4.8 %all-to-all-start.1 = ((f32[8,2,8,128]{3,2,1,0:T(8,128)}), f32[8,2,8,128]{3,2,1,0:T(8,128)S(1)}, u32[]{:S(2)}, u32[]{:S(2)}) async-start(f32[8,2,8,128]{3,2,1,0:T(8,128)} %green.1), calls=%async_computation.1 | async-start | bytes 131072 | tf_op jit(solution)/shard_map/all_to_all | solution.py:800
  28.8 0.0 copy-start.1
  28.8 0.0 copy-start.2
  28.8 7.1 %muscl_early.1.refs_6_ = f32[4,8192,128]{2,1,0:T(8,128)} custom-call(f32[4,8192,128]{2,1,0:T(8,128)} %bitcast.28), custom_call_target="tpu_custom_call" | custom-call | flops 196608000 | bytes 4194304 | tf_op jit(solution)/shard_map/muscl_early/pallas_call | solution.py:734
  35.9 0.0 collective-permute-done.1
  35.9 0.0 collective-permute-done
  35.9 0.0 all-to-all-done.1.refs_3_
  35.9 0.0 copy-done.1
  35.9 0.0 copy-done.2
  35.9 34.4 %muscl_final.1 = (f32[4,8192,128]{2,1,0:T(8,128)}, f32[8192,128]{1,0:T(8,128)}) custom-call(f32[4,8192,128]{2,1,0:T(8,128)} %bitcast.29, f32[4,128,128]{2,1,0:T(8,128)S(1)} %bitcast.24, f32[4,128,128]{2,1,0:T(8,128)S(1)} %bitcast.23, f32[8,2,8,128]{3,2,1,0:T(8,128)S(1)} %all-to-all-done.1.refs_3_, ...), custom_call_target="tpu_custom_call", output_to_operand_aliasing={{0}: (6, {})} | custom-call | flops 1376256000 | bytes 29360128 | tf_op jit(solution)/shard_map/muscl_final/pallas_call | solution.py:734
  (2 shorter events, 0.0 us)
Async XLA Ops:
  0.6 19.1 %copy-start = (f32[16,16]{1,0:T(8,128)S(1)}, f32[16,16]{1,0:T(8,128)}, u32[]{:S(2)}) copy-start(f32[16,16]{1,0:T(8,128)} %param.8) | copy-start | bytes 3076
  5.4 15.5 %all-to-all-start = ((f32[32,8,128]{2,1,0:T(8,128)}), f32[32,8,128]{2,1,0:T(8,128)S(1)}, u32[]{:S(2)}, u32[]{:S(2)}) async-start(f32[32,8,128]{2,1,0:T(8,128)} %bitcast.31), calls=%async_computation | async-start | bytes 262144 | tf_op jit(solution)/shard_map/all_to_all | solution.py:783
  13.8 22.1 %collective-permute-start.1 = (f32[4,2,64,128]{3,2,1,0:T(8,128)S(1)}, f32[4,2,64,128]{3,2,1,0:T(8,128)S(1)}, u32[]{:S(2)}, u32[]{:S(2)}) collective-permute-start(f32[4,2,64,128]{3,2,1,0:T(8,128)S(1)} %get-tuple-element.6), channel_id=1, source_target_pairs={{4,0},{8,4},{12,8},{16,12},{20,16},{24,20},{28,24},{5,1},{9,5},{13... | collective-permute-start | bytes 786440 | tf_op jit(solution)/shard_map/ppermute | solution.py:765
  15.1 20.8 %collective-permute-start = (f32[4,2,64,128]{3,2,1,0:T(8,128)S(1)}, f32[4,2,64,128]{3,2,1,0:T(8,128)S(1)}, u32[]{:S(2)}, u32[]{:S(2)}) collective-permute-start(f32[4,2,64,128]{3,2,1,0:T(8,128)S(1)} %get-tuple-element.7), channel_id=1, source_target_pairs={{0,4},{4,8},{8,12},{12,16},{16,20},{20,24},{24,28},{1,5},{5,9},{9,... | collective-permute-start | bytes 786440 | tf_op jit(solution)/shard_map/ppermute | solution.py:764
  20.9 1.6 %copy-start.3 = (bf16[1,1024,1024]{2,1,0:T(8,128)(2,1)S(1)}, bf16[1,1024,1024]{2,1,0:T(8,128)(2,1)}, u32[]{:S(2)}) copy-start(bf16[1,1024,1024]{2,1,0:T(8,128)(2,1)} %green_ref.1) | copy-start | bytes 6291460
  24.0 11.9 %all-to-all-start.1 = ((f32[8,2,8,128]{3,2,1,0:T(8,128)}), f32[8,2,8,128]{3,2,1,0:T(8,128)S(1)}, u32[]{:S(2)}, u32[]{:S(2)}) async-start(f32[8,2,8,128]{3,2,1,0:T(8,128)} %green.1), calls=%async_computation.1 | async-start | bytes 131072 | tf_op jit(solution)/shard_map/all_to_all | solution.py:800
  28.8 7.1 %copy-start.1 = (bf16[256,1024]{1,0:T(8,128)(2,1)S(1)}, bf16[256,1024]{1,0:T(8,128)(2,1)}, u32[]{:S(2)}) copy-start(bf16[256,1024]{1,0:T(8,128)(2,1)} %constant.18.clone.refs_5_) | copy-start | bytes 1572868
  28.8 7.1 %copy-start.2 = (bf16[256,1024]{1,0:T(8,128)(2,1)S(1)}, bf16[256,1024]{1,0:T(8,128)(2,1)}, u32[]{:S(2)}) copy-start(bf16[256,1024]{1,0:T(8,128)(2,1)} %constant.17.clone.refs_4_) | copy-start | bytes 1572868
